TPU v7x, 512 devices: a whole 4x4x16 slice. The times are simulated.
512 devices in a mesh: leaf: 16 (over z_lo, core), grp: 8 (over y, z_hi), mrg: 4 (over x).
Axes of the slice: x: 4, y: 4, z: 16 (z_hi: 2, z_lo: 8; z = z_hi * 8 + z_lo), core: 2. Of those that a mesh axis runs over, the one named last changes fastest.
Arguments:
- row_owner: int32 [768], replicated, may hold values from 0 to 767, as said below
- face_left: float32 [8, 4, 768, 768], P('grp', 'mrg', 'leaf'), as said below
- face_cross: float32 [8, 4, 768, 768], P('grp', 'mrg', 'leaf')
- face_right: float32 [8, 4, 768, 768], P('grp', 'mrg', 'leaf')
Outputs:
- out_left: float32 [8, 4, 768, 768], P('grp', 'mrg', 'leaf')
- out_cross: float32 [8, 4, 768, 768], P('grp', 'mrg', 'leaf')
- out_right: float32 [8, 4, 768, 768], P('grp', 'mrg', 'leaf')
Inputs may be any that keep to these rules, and one draw needn't show every extreme that they name: row_owner holds each of the 768 face DOFs exactly once. `face_left`: for every box, the symmetric matrix [[L, C], [C^T, R]] built from natural rows is positive definite, L and R are symmetric.
All inputs are finite; a program needn't handle non-finite values.
Results may differ from a plain program's by a relative error of at most 0.0003.
Values sent between devices are 32-bit elements; how exact they have to be, the bound alone decides.
No kernel may reach another device: no remote copies, remote signals or barrier semaphores. Data moves between devices by JAX's collectives and lax.ppermute only.
A program may use at most 128 MiB of HBM per device.

v0:
```python
import jax
import jax.numpy as jnp
from jax import lax
from jax.sharding import PartitionSpec as P


def partner_2(block, axis, distance):
    count = lax.axis_size(axis)
    route = []
    for low in range(count):
        high = low | 1 << distance
        if high != low and high < count:
            route += [(low, high), (high, low)]
    return lax.ppermute(block, axis, route)


def dot_high(left, right):
    return jnp.dot(left, right, precision=lax.Precision.HIGHEST, preferred_element_type=jnp.float32)


def dot_against(left, right):
    return lax.dot_general(
        left,
        right,
        (((1,), (1,)), ((), ())),
        precision=lax.Precision.HIGHEST,
        preferred_element_type=jnp.float32,
    )


def dot_leading(left, right):
    return lax.dot_general(
        left,
        right,
        (((0,), (0,)), ((), ())),
        precision=lax.Precision.HIGHEST,
        preferred_element_type=jnp.float32,
    )


def arrange(mine, partner, role):
    first = jnp.where(role == 0, mine, partner)
    second = jnp.where(role == 0, partner, mine)
    return (first, second)


def merge_rows(first, second, factor, cross_left, cross_right, start):
    rows = first.shape[1]
    columns = lax.dynamic_slice_in_dim(cross_right, start, rows, 1)
    solved = jax.scipy.linalg.cho_solve((factor, True), first[1].T).T
    weights = jax.scipy.linalg.cho_solve((factor, True), columns)
    new_left = first[0] - dot_against(solved, cross_left)
    new_cross = -dot_high(solved, cross_right)
    new_right = second[2] - dot_leading(weights, cross_right)
    return jnp.stack([new_left, new_cross, new_right])


def shards(row_owner, face_left, face_cross, face_right):
    rows = face_left.shape[2]
    width = face_left.shape[3]
    mine = jnp.stack([face_left[0, 0], face_cross[0, 0], face_right[0, 0]])
    mine = jnp.take(mine, row_owner, axis=2)
    inverse_map = (
        jnp.zeros((width,), jnp.int32).at[row_owner].set(jnp.arange(width, dtype=jnp.int32))
    )
    start = lax.axis_index("leaf") * rows
    role_one = lax.axis_index("grp") % 2
    partner = partner_2(mine, "grp", 0)
    first, second = arrange(mine, partner, role_one)
    gathered = lax.all_gather(
        jnp.stack([first[2] + second[0], first[1], second[1]]), "leaf", axis=1, tiled=True
    )
    factor = jnp.linalg.cholesky(gathered[0])
    crossing = gathered[1:]
    mine = merge_rows(first, second, factor, crossing[0], crossing[1], start)
    role_two = lax.axis_index("mrg") % 2
    partner = partner_2(mine, "mrg", 0)
    first, second = arrange(mine, partner, role_two)
    gathered = lax.all_gather(
        jnp.stack([first[2] + second[0], first[1], second[1]]), "leaf", axis=1, tiled=True
    )
    factor = jnp.linalg.cholesky(gathered[0])
    crossing = gathered[1:]
    mine = merge_rows(first, second, factor, crossing[0], crossing[1], start)
    mine = jnp.take(mine, inverse_map, axis=2)
    return (mine[0][None, None], mine[1][None, None], mine[2][None, None])


def solution(mesh):
    in_specs = (
        P(),
        P("grp", "mrg", "leaf", None),
        P("grp", "mrg", "leaf", None),
        P("grp", "mrg", "leaf", None),
    )
    out_specs = (
        P("grp", "mrg", "leaf", None),
        P("grp", "mrg", "leaf", None),
        P("grp", "mrg", "leaf", None),
    )
    return jax.shard_map(shards, mesh=mesh, in_specs=in_specs, out_specs=out_specs, check_vma=False)
```

profile of v0, /device:TPU:24, one launch (start us, length us, event | category | flops | bytes accessed | tf_op | source)
XLA Modules:
  0.0 837.0 jit_solution(3703308753409520388)
XLA Ops:
  10.4 3.4 scatter_custom_fusion
  13.8 2.8 gather_fusion
  17.2 15.7 %collective-permute-start = (f32[3,48,768]{2,1,0:T(8,128)S(1)}, f32[3,48,768]{2,1,0:T(8,128)S(1)}, u32[]{:S(2)}, u32[]{:S(2)}) collective-permute-start(f32[3,48,768]{2,1,0:T(8,128)S(1)} %select_bitcast_fusion.1), channel_id=1, source_target_pairs={{0,4},{4,0},{8,12},{12,8},{16,20},{20,16},{24,28},{28,24},{1,5},{5... | collective-permute-start | bytes 1327112 | tf_op jit(solution)/shard_map/ppermute | solution.py:14
  33.0 14.7 %collective-permute-done = f32[3,48,768]{2,1,0:T(8,128)S(1)} collective-permute-done((f32[3,48,768]{2,1,0:T(8,128)S(1)}, f32[3,48,768]{2,1,0:T(8,128)S(1)}, u32[]{:S(2)}, u32[]{:S(2)}) %collective-permute-start) | collective-permute-done | bytes 442400 | tf_op jit(solution)/shard_map/ppermute | solution.py:14
  49.6 137.9 %all-gather.3.cloned.1.call-done = f32[3,768,768]{2,1,0:T(8,128)} async-done(((f32[3,48,768]{2,1,0:T(8,128)}), f32[3,768,768]{2,1,0:T(8,128)}) %all-gather.3.cloned.1.call-update) | async-done | bytes 7077904 | tf_op jit(solution)/shard_map/all_gather | solution.py:70
  187.5 4.1 fusion.325
  192.6 2.5 copy.46
  195.1 2.0 fusion.3
  198.6 11.7 %cholesky.453 = f32[128,128]{1,0:T(8,128)S(1)} custom-call(f32[128,128]{1,0:T(8,128)S(1)} %cholesky.669), custom_call_target="Cholesky" | custom-call | tf_op jit(solution)/shard_map/jit(cholesky)/cholesky | solution.py:73
  210.5 9.8 %custom-call.45 = f32[1,128,128]{1,2,0:T(8,128)S(1)} custom-call(f32[1,128,128]{2,1,0:T(8,128)S(1)} %get-tuple-element.115), custom_call_target="InvertDiagBlocksLowerTriangular" | custom-call | tf_op jit(solution)/shard_map/jit(cholesky)/cholesky | solution.py:73
  223.1 11.7 %cholesky.472 = f32[128,128]{1,0:T(8,128)S(1)} custom-call(f32[128,128]{1,0:T(8,128)S(1)} %cholesky.673), custom_call_target="Cholesky" | custom-call | tf_op jit(solution)/shard_map/jit(cholesky)/cholesky | solution.py:73
  234.8 10.0 %custom-call.46 = f32[1,128,128]{1,2,0:T(8,128)S(1)} custom-call(f32[1,128,128]{2,1,0:T(8,128)S(1)} %get-tuple-element.112), custom_call_target="InvertDiagBlocksLowerTriangular" | custom-call | tf_op jit(solution)/shard_map/jit(cholesky)/cholesky | solution.py:73
  246.7 11.7 %cholesky.493 = f32[128,128]{1,0:T(8,128)S(1)} custom-call(f32[128,128]{1,0:T(8,128)S(1)} %cholesky.678), custom_call_target="Cholesky" | custom-call | tf_op jit(solution)/shard_map/jit(cholesky)/cholesky | solution.py:73
  258.5 9.8 %custom-call.47 = f32[1,128,128]{1,2,0:T(8,128)S(1)} custom-call(f32[1,128,128]{2,1,0:T(8,128)S(1)} %get-tuple-element.109), custom_call_target="InvertDiagBlocksLowerTriangular" | custom-call | tf_op jit(solution)/shard_map/jit(cholesky)/cholesky | solution.py:73
  268.6 1.6 convolution_subtract_fusion.5
  270.2 12.1 %cholesky.512 = f32[128,128]{1,0:T(8,128)S(1)} custom-call(f32[128,128]{1,0:T(8,128)S(1)} %cholesky.683), custom_call_target="Cholesky" | custom-call | tf_op jit(solution)/shard_map/jit(cholesky)/cholesky | solution.py:73
  282.3 9.8 %custom-call.48 = f32[1,128,128]{1,2,0:T(8,128)S(1)} custom-call(f32[1,128,128]{2,1,0:T(8,128)S(1)} %get-tuple-element.106), custom_call_target="InvertDiagBlocksLowerTriangular" | custom-call | tf_op jit(solution)/shard_map/jit(cholesky)/cholesky | solution.py:73
  293.9 11.7 %cholesky.531 = f32[128,128]{1,0:T(8,128)S(1)} custom-call(f32[128,128]{1,0:T(8,128)S(1)} %cholesky.688), custom_call_target="Cholesky" | custom-call | tf_op jit(solution)/shard_map/jit(cholesky)/cholesky | solution.py:73
  305.7 9.8 %custom-call.49 = f32[1,128,128]{1,2,0:T(8,128)S(1)} custom-call(f32[1,128,128]{2,1,0:T(8,128)S(1)} %get-tuple-element.103), custom_call_target="InvertDiagBlocksLowerTriangular" | custom-call | tf_op jit(solution)/shard_map/jit(cholesky)/cholesky | solution.py:73
  317.0 11.9 %cholesky.548 = f32[128,128]{1,0:T(8,128)S(1)} custom-call(f32[128,128]{1,0:T(8,128)S(1)} %convolution_subtract_fusion.9), custom_call_target="Cholesky" | custom-call | tf_op jit(solution)/shard_map/jit(cholesky)/cholesky | solution.py:73
  336.9 3.4 select_select_fusion.1
  340.3 17.9 %while.8 = (s32[]{:T(128)}, f32[768,768]{1,0:T(8,128)}, s32[6,2]{0,1:T(2,128)S(1)}, f32[6,128,128]{2,1,0:T(8,128)S(1)}, s32[]{:T(128)}) while((s32[]{:T(128)}, f32[768,768]{1,0:T(8,128)}, s32[6,2]{0,1:T(2,128)S(1)}, f32[6,128,128]{2,1,0:T(8,128)S(1)}, s32[]{:T(128)}) %tuple.109), condition=%wide.while_cond, body=%wide.while_body.sunk | while | flops 2 | bytes 131189 | solution.py:50
  341.0 2.3 bitcast_dynamic-update-slice_fusion.4
  344.0 2.3 bitcast_dynamic-update-slice_fusion.4
  347.0 2.3 bitcast_dynamic-update-slice_fusion.4
  350.0 2.3 bitcast_dynamic-update-slice_fusion.4
  353.0 2.3 bitcast_dynamic-update-slice_fusion.4
  356.0 2.2 bitcast_dynamic-update-slice_fusion.4
  359.0 59.8 %custom-call.50 = f32[6,128,128]{1,2,0:T(8,128)S(1)} custom-call(f32[6,128,128]{2,1,0:T(8,128)} %copy-done.11), custom_call_target="InvertDiagBlocksLowerTriangular" | custom-call | tf_op jit(solution)/shard_map/jit(_cho_solve)/triangular_solve | solution.py:50
  425.5 1.6 convolution_subtract_fusion.36
  437.2 3.2 fusion.81
  440.4 2.4 fusion.79
  442.9 3.3 collective-permute-start.1
  446.2 6.9 collective-permute-done.1
  454.9 109.9 %all-gather.5.cloned.1.call-done = f32[3,768,768]{2,1,0:T(8,128)} async-done(((f32[3,48,768]{2,1,0:T(8,128)}), f32[3,768,768]{2,1,0:T(8,128)}) %all-gather.5.cloned.1.call-update) | async-done | bytes 7077904 | tf_op jit(solution)/shard_map/all_gather | solution.py:79
  564.9 4.1 fusion.324
  570.0 2.4 copy.47
  572.5 2.0 fusion.2
  575.9 11.7 %cholesky.563 = f32[128,128]{1,0:T(8,128)S(1)} custom-call(f32[128,128]{1,0:T(8,128)S(1)} %cholesky.692), custom_call_target="Cholesky" | custom-call | tf_op jit(solution)/shard_map/jit(cholesky)/cholesky | solution.py:82
  587.8 9.8 %custom-call.52 = f32[1,128,128]{1,2,0:T(8,128)S(1)} custom-call(f32[1,128,128]{2,1,0:T(8,128)S(1)} %get-tuple-element.99), custom_call_target="InvertDiagBlocksLowerTriangular" | custom-call | tf_op jit(solution)/shard_map/jit(cholesky)/cholesky | solution.py:82
  600.4 11.7 %cholesky.582 = f32[128,128]{1,0:T(8,128)S(1)} custom-call(f32[128,128]{1,0:T(8,128)S(1)} %cholesky.696), custom_call_target="Cholesky" | custom-call | tf_op jit(solution)/shard_map/jit(cholesky)/cholesky | solution.py:82
  612.2 10.0 %custom-call.53 = f32[1,128,128]{1,2,0:T(8,128)S(1)} custom-call(f32[1,128,128]{2,1,0:T(8,128)S(1)} %get-tuple-element.96), custom_call_target="InvertDiagBlocksLowerTriangular" | custom-call | tf_op jit(solution)/shard_map/jit(cholesky)/cholesky | solution.py:82
  624.0 11.7 %cholesky.603 = f32[128,128]{1,0:T(8,128)S(1)} custom-call(f32[128,128]{1,0:T(8,128)S(1)} %cholesky.701), custom_call_target="Cholesky" | custom-call | tf_op jit(solution)/shard_map/jit(cholesky)/cholesky | solution.py:82
  635.8 9.8 %custom-call.54 = f32[1,128,128]{1,2,0:T(8,128)S(1)} custom-call(f32[1,128,128]{2,1,0:T(8,128)S(1)} %get-tuple-element.93), custom_call_target="InvertDiagBlocksLowerTriangular" | custom-call | tf_op jit(solution)/shard_map/jit(cholesky)/cholesky | solution.py:82
  645.9 1.6 convolution_subtract_fusion.4
  647.5 12.1 %cholesky.622 = f32[128,128]{1,0:T(8,128)S(1)} custom-call(f32[128,128]{1,0:T(8,128)S(1)} %cholesky.706), custom_call_target="Cholesky" | custom-call | tf_op jit(solution)/shard_map/jit(cholesky)/cholesky | solution.py:82
  659.6 9.8 %custom-call.55 = f32[1,128,128]{1,2,0:T(8,128)S(1)} custom-call(f32[1,128,128]{2,1,0:T(8,128)S(1)} %get-tuple-element.90), custom_call_target="InvertDiagBlocksLowerTriangular" | custom-call | tf_op jit(solution)/shard_map/jit(cholesky)/cholesky | solution.py:82
  671.2 11.7 %cholesky.641 = f32[128,128]{1,0:T(8,128)S(1)} custom-call(f32[128,128]{1,0:T(8,128)S(1)} %cholesky.711), custom_call_target="Cholesky" | custom-call | tf_op jit(solution)/shard_map/jit(cholesky)/cholesky | solution.py:82
  683.0 9.8 %custom-call.56 = f32[1,128,128]{1,2,0:T(8,128)S(1)} custom-call(f32[1,128,128]{2,1,0:T(8,128)S(1)} %get-tuple-element.87), custom_call_target="InvertDiagBlocksLowerTriangular" | custom-call | tf_op jit(solution)/shard_map/jit(cholesky)/cholesky | solution.py:82
  694.3 11.7 %cholesky.658 = f32[128,128]{1,0:T(8,128)S(1)} custom-call(f32[128,128]{1,0:T(8,128)S(1)} %convolution_subtract_fusion.8), custom_call_target="Cholesky" | custom-call | tf_op jit(solution)/shard_map/jit(cholesky)/cholesky | solution.py:82
  714.1 3.4 select_select_fusion
  717.5 18.1 %while.9 = (s32[]{:T(128)}, f32[768,768]{1,0:T(8,128)}, s32[6,2]{0,1:T(2,128)S(1)}, f32[6,128,128]{2,1,0:T(8,128)S(1)}, s32[]{:T(128)}) while((s32[]{:T(128)}, f32[768,768]{1,0:T(8,128)}, s32[6,2]{0,1:T(2,128)S(1)}, f32[6,128,128]{2,1,0:T(8,128)S(1)}, s32[]{:T(128)}) %tuple.119), condition=%wide.while_cond.clone.1, body=%wide.while_body.clone.1.sunk | while | flops 2 | bytes 131189 | solution.py:50
  718.2 2.3 bitcast_dynamic-update-slice_fusion.5
  721.2 2.3 bitcast_dynamic-update-slice_fusion.5
  724.2 2.3 bitcast_dynamic-update-slice_fusion.5
  727.3 2.3 bitcast_dynamic-update-slice_fusion.5
  730.3 2.3 bitcast_dynamic-update-slice_fusion.5
  733.3 2.3 bitcast_dynamic-update-slice_fusion.5
  736.3 59.9 %custom-call.57 = f32[6,128,128]{1,2,0:T(8,128)S(1)} custom-call(f32[6,128,128]{2,1,0:T(8,128)} %copy-done.10), custom_call_target="InvertDiagBlocksLowerTriangular" | custom-call | tf_op jit(solution)/shard_map/jit(_cho_solve)/triangular_solve | solution.py:50
  803.0 1.6 convolution_subtract_fusion.30
  814.8 3.2 fusion.77
  818.0 2.4 fusion.75
  821.1 2.8 gather_fusion.1
  824.0 2.8 select_bitcast_fusion
  (271 shorter events, 84.2 us)
Async XLA Ops:
  7.2 180.3 %all-gather.3.cloned.1.call-start = ((), (), s32[]{:S(2)}) async-start(), calls=%async_computation | async-start | bytes 7520256 | tf_op jit(solution)/shard_map/all_gather | solution.py:70
  17.2 30.4 %collective-permute-start = (f32[3,48,768]{2,1,0:T(8,128)S(1)}, f32[3,48,768]{2,1,0:T(8,128)S(1)}, u32[]{:S(2)}, u32[]{:S(2)}) collective-permute-start(f32[3,48,768]{2,1,0:T(8,128)S(1)} %select_bitcast_fusion.1), channel_id=1, source_target_pairs={{0,4},{4,0},{8,12},{12,8},{16,20},{20,16},{24,28},{28,24},{1,5},{5... | collective-permute-start | bytes 1327112 | tf_op jit(solution)/shard_map/ppermute | solution.py:14
  47.8 0.8 copy-start.6
  47.8 0.9 copy-start.7
  49.5 515.4 %all-gather.5.cloned.1.call-start = ((), (), s32[]{:S(2)}) async-start(), calls=%async_computation.1 | async-start | bytes 7520256 | tf_op jit(solution)/shard_map/all_gather | solution.py:79
  197.1 1.5 copy-start.4
  328.9 8.0 copy-start
  336.9 98.8 %slice-start = ((s8[7077888]{0:T(1024)(128)(4,1)}), s8[2883584]{0:T(1024)(128)(4,1)S(1)}, s32[]{:S(2)}) async-start(s8[7077888]{0:T(1024)(128)(4,1)} %bitcast.376), calls=%async_computation.2 | async-start | bytes 5767168
  358.2 0.7 copy-start.11
  418.7 8.7 %copy-start.3 = (f32[768,768]{1,0:T(8,128)S(1)}, f32[768,768]{1,0:T(8,128)}, u32[]{:S(2)}) copy-start(f32[768,768]{1,0:T(8,128)} %get-tuple-element.263) | copy-start | bytes 7077892
  425.5 10.2 %slice-start.1 = ((s8[7077888]{0:T(1024)(128)(4,1)}), s8[4194304]{0:T(1024)(128)(4,1)S(1)}, s32[]{:S(2)}) async-start(s8[7077888]{0:T(1024)(128)(4,1)} %bitcast.376), calls=%async_computation.3 | async-start | bytes 8388608
  442.9 10.2 %collective-permute-start.1 = (f32[3,48,768]{2,1,0:T(8,128)S(1)}, f32[3,48,768]{2,1,0:T(8,128)S(1)}, u32[]{:S(2)}, u32[]{:S(2)}) collective-permute-start(f32[3,48,768]{2,1,0:T(8,128)S(1)} %pad_maximum_fusion.2), channel_id=1, source_target_pairs={{0,1},{1,0},{2,3},{3,2},{4,5},{5,4},{6,7},{7,6},{8,9},{9,8},{10,11... | collective-permute-start | bytes 1327112 | tf_op jit(solution)/shard_map/ppermute | solution.py:14
  453.2 0.8 copy-start.8
  453.2 0.9 copy-start.9
  574.4 1.5 copy-start.5
  706.1 8.0 copy-start.1
  714.1 99.2 %slice-start.2 = ((s8[7077888]{0:T(1024)(128)(4,1)}), s8[2883584]{0:T(1024)(128)(4,1)S(1)}, s32[]{:S(2)}) async-start(s8[7077888]{0:T(1024)(128)(4,1)} %bitcast.378), calls=%async_computation.4 | async-start | bytes 5767168
  735.6 0.7 copy-start.10
  796.3 8.7 %copy-start.2 = (f32[768,768]{1,0:T(8,128)S(1)}, f32[768,768]{1,0:T(8,128)}, u32[]{:S(2)}) copy-start(f32[768,768]{1,0:T(8,128)} %get-tuple-element.262) | copy-start | bytes 7077892
  803.0 10.2 %slice-start.3 = ((s8[7077888]{0:T(1024)(128)(4,1)}), s8[4194304]{0:T(1024)(128)(4,1)S(1)}, s32[]{:S(2)}) async-start(s8[7077888]{0:T(1024)(128)(4,1)} %bitcast.378), calls=%async_computation.5 | async-start | bytes 8388608
Sparse Core Ops, SparseCore 0:
  49.6 137.8 all-gather.2
  455.0 109.7 all-gather.4
where the time goes:
time: 842 us; the launch traced here: 837 us
  other arithmetic  386 us (46%)
  waiting for transfers between devices  269 us (32%)
  local copies, waits for them, and re-layouts  71.9 us (9%)
  matrix products  66.5 us (8%)
  between operations  23.6 us (3%)
  starting transfers between devices  19.1 us (2%)
    another operation x46, other arithmetic, shards(): factor = jnp.linalg.cholesky(gathered[0])  249 us
    all_gather x2, waiting for transfers between devices, shards(): lax.all_gather(jnp.stack([first[2] + second[0], first[1], second[1]]), 'l...  248 us
    another operation x5, other arithmetic, merge_rows(): solved = jax.scipy.linalg.cho_solve((factor, True), first[1].T).T  126 us
    another operation x43, local copies, waits for them, and re-layouts, merge_rows(): solved = jax.scipy.linalg.cho_solve((factor, True), first[1].T).T  35.8 us
    another operation x44, matrix products, merge_rows(): weights = jax.scipy.linalg.cho_solve((factor, True), columns)  22 us
    ppermute x2, waiting for transfers between devices, partner_2(): return lax.ppermute(block, axis, route)  21.6 us
    another operation x20, matrix products, shards(): factor = jnp.linalg.cholesky(gathered[0])  19.6 us
    ppermute x2, starting transfers between devices, partner_2(): return lax.ppermute(block, axis, route)  19 us
  transfers between devices with their start and end apart: 4, of which 4 were waited for; matrix products, arithmetic and copies ran while one was open for 0% of the time, Pallas kernels for 0%

commit v1 on v0

v1 whole, which is shorter than its diff:
```python
import functools

import jax
import jax.numpy as jnp
from jax import lax
from jax.experimental import pallas as pl
from jax.experimental.pallas import tpu as pltpu
from jax.sharding import Mesh
from jax.sharding import PartitionSpec as P

F = 768
ROWS = 48
HALF = 384
B = 128
F32 = jnp.float32
BF16 = jnp.bfloat16
PAIR = ("zh", "zl", "core")
SWAP = [(0, 1), (1, 0)]
VMEM = pl.BlockSpec(memory_space=pltpu.VMEM)
ANY = pl.BlockSpec(memory_space=pl.ANY)


def params(mib):
    return pltpu.CompilerParams(vmem_limit_bytes=mib * 1024 * 1024)


def dg(a, b, dims):
    return lax.dot_general(a, b, (dims, ((), ())), preferred_element_type=F32)


NN = ((1,), (0,))
NT = ((1,), (1,))
TN = ((0,), (0,))
TT = ((0,), (1,))


def split2(x):
    h = x.astype(BF16)
    return h, (x - h.astype(F32)).astype(BF16)


def split3(x):
    h = x.astype(BF16)
    y = x - h.astype(F32)
    m = y.astype(BF16)
    return h, m, (y - m.astype(F32)).astype(BF16)


def mul3(a, b, dims):
    return (dg(a[1], b[0], dims) + dg(a[0], b[1], dims)) + dg(a[0], b[0], dims)


def pick(x, onehot, dims):
    h, m, l = split3(x)
    return (dg(l, onehot, dims) + dg(m, onehot, dims)) + dg(h, onehot, dims)


def onehot_of(ro):
    c = lax.broadcasted_iota(jnp.int32, (F, F), 0)
    return jnp.where(c == ro, 1.0, 0.0).astype(BF16)


def sub(v, s):
    return jnp.broadcast_to(v[s : s + 1, :], v.shape)


def lane(v, j):
    return jnp.broadcast_to(v[:, j : j + 1], v.shape)


def inv8(b, row):
    b = list(b)
    for p in range(4):
        i, k = 2 * p, 2 * p + 1
        a_, b_, d_ = sub(b[i], i), sub(b[k], i), sub(b[k], k)
        rd = 1.0 / (a_ * d_ - b_ * b_)
        pa, pb, pd = d_ * rd, -b_ * rd, a_ * rd
        ci = jnp.where(row == i, -1.0, jnp.where(row == k, 0.0, b[i]))
        ck = jnp.where(row == k, -1.0, jnp.where(row == i, 0.0, b[k]))
        ui = ci * pa + ck * pb
        uk = ci * pb + ck * pd
        keep = (row != i) & (row != k)
        new = []
        for j in range(8):
            if j == i:
                new.append(-ui)
            elif j == k:
                new.append(-uk)
            else:
                base = jnp.where(keep, b[j], 0.0)
                new.append(base - (ui * sub(b[j], i) + uk * sub(b[j], k)))
        b = new
    return b


def tree(u):
    return ((u[0] + u[1]) + (u[2] + u[3])) + ((u[4] + u[5]) + (u[6] + u[7]))


def inv128(D):
    row = lax.broadcasted_iota(jnp.int32, (8, B), 0)
    col = lax.broadcasted_iota(jnp.int32, (8, B), 1)
    D = list(D)
    for r in range(16):
        rows = D[r]
        ib = inv8([lane(rows, 8 * r + j) for j in range(8)], row)
        inp = (col >= 8 * r) & (col < 8 * r + 8)
        rows = jnp.where(inp, jnp.where(col - 8 * r == row, 1.0, 0.0), rows)
        T = tree([ib[j] * sub(rows, j) for j in range(8)])
        Tj = [sub(T, j) for j in range(8)]
        for q in list(range(r + 1, 16)) + list(range(r)):
            u = tree([lane(D[q], 8 * r + j) * Tj[j] for j in range(8)])
            D[q] = jnp.where(inp, 0.0, D[q]) - u
        D[r] = T
    return D


def cat(*a, axis):
    return jnp.concatenate(a, axis=axis)


def mul6(a, b):
    a0, a1, a2 = split3(a)
    b0, b1, b2 = split3(b)
    a01 = cat(a0, a1, axis=1)
    low = dg(cat(a0, a2, axis=1), cat(b2, b0, axis=0), NN) + dg(a01, cat(b1, b1, axis=0), NN)
    return low + dg(a01, cat(b0, b0, axis=0), NN)


def invert(s_ref, d_ref, di_ref, r_ref, c_ref):
    ri = lax.broadcasted_iota(jnp.int32, (B, B), 0)
    ci = lax.broadcasted_iota(jnp.int32, (B, B), 1)
    eye = jnp.where(ri == ci, 1.0, 0.0)
    last = F // B - 1
    di_ref[...] = jnp.zeros((B, B), F32)
    r_ref[...] = jnp.zeros((B, F), F32)
    c_ref[...] = jnp.zeros((F, B), F32)
    d_ref[...] = s_ref[:B, :B]

    def trail(kp):
        T = mul6(di_ref[...], r_ref[...])
        t0, t1 = split2(T)
        c0, c1 = split2(c_ref[...])
        lhs = cat(c0, c1, axis=1)
        rhs = cat(t0, t0, axis=0)
        for j in range(F // 256):
            js = slice(256 * j, 256 * j + 256)
            s_ref[:F, js] = s_ref[:F, js] - (dg(lhs, rhs[:, js], NN) + dg(c0, t1[:, js], NN))
        s_ref[pl.ds(kp, B), :] = T

    def step(k, carry):
        ks = pl.multiple_of(k * B, B)
        kp = pl.multiple_of(jnp.where(k == 0, F, ks - B), B)
        kn = pl.multiple_of(jnp.where(k == last, F - B, ks + B), B)
        Di = jnp.concatenate(inv128([d_ref[8 * q : 8 * q + 8, :] for q in range(16)]), axis=0)
        trail(kp)
        rn = s_ref[pl.ds(ks, B), pl.ds(kn, B)]
        cn = s_ref[pl.ds(kn, B), pl.ds(ks, B)]
        dn = s_ref[pl.ds(kn, B), pl.ds(kn, B)]
        c_ref[...] = s_ref[:F, pl.ds(ks, B)]
        c_ref[pl.ds(ks, B), :] = jnp.zeros((B, B), F32)
        r_ref[...] = s_ref[pl.ds(ks, B), :]
        r_ref[:, pl.ds(ks, B)] = eye
        s_ref[:F, pl.ds(ks, B)] = jnp.zeros((F, B), F32)
        di_ref[...] = Di
        t0, t1 = split2(mul6(Di, rn))
        c0, c1 = split2(cn)
        d_ref[...] = dn - (dg(cat(c0, c1, axis=1), cat(t0, t0, axis=0), NN) + dg(c0, t1, NN))
        return carry

    lax.fori_loop(0, last + 1, step, 0)
    trail(F - B)


INVERT_SCRATCH = [
    pltpu.VMEM((F + B, F), F32),
    pltpu.VMEM((B, B), F32),
    pltpu.VMEM((B, B), F32),
    pltpu.VMEM((B, F), F32),
    pltpu.VMEM((F, B), F32),
]


def enter_body(ro, left, cross, right, send, other):
    p = onehot_of(ro[...])
    upper = lax.axis_index("zh") == 1
    l, c, r = left[...], cross[...], right[...]
    send[0] = pick(jnp.where(upper, l, r), p, NN)
    send[1] = pick(c, p, NN)
    other[...] = pick(jnp.where(upper, r, l), p, NN)


def enter(ro, left, cross, right):
    return pl.pallas_call(
        enter_body,
        out_shape=(jax.ShapeDtypeStruct((2, ROWS, F), F32), jax.ShapeDtypeStruct((ROWS, F), F32)),
        in_specs=[VMEM] * 4,
        out_specs=(VMEM, VMEM),
        compiler_params=params(32),
        name="enter",
    )(ro, left, cross, right)


def level_one_body(g, v_out, t_out, si_out, a_ref, c_ref, t_ref, sems, s_ref, *work):
    ga = pltpu.make_async_copy(g.at[0], a_ref, sems.at[0])
    gc = pltpu.make_async_copy(g.at[1], c_ref, sems.at[1])
    ga.start()
    gc.start()
    ga.wait()
    s_ref[:F, :] = a_ref[:F, :] + a_ref[F:, :]
    invert(s_ref, *work)
    gc.wait()
    si_out[...] = s_ref[:F, :]
    si = split2(s_ref[:F, :])
    h = pl.multiple_of(lax.axis_index("core") * HALF, HALF)
    low = lax.axis_index("xl") == 0

    @pl.when(low)
    def _():
        cb = split2(c_ref[F:, :])
        t = mul3(si, cb, NN)
        t_out[...] = t
        part = split2(c_ref[F:, pl.ds(h, HALF)])
        v_out[...] = mul3(part, split2(t), TN)

    @pl.when(jnp.logical_not(low))
    def _():
        ca = split2(c_ref[:F, :])
        t_ref[...] = mul3(ca, si, NN)
        t_out[...] = t_ref[...]
        part = split2(t_ref[pl.ds(h, HALF), :])
        v_out[...] = mul3(part, ca, NT)


def level_one(g):
    mat = jax.ShapeDtypeStruct((F, F), F32)
    return pl.pallas_call(
        level_one_body,
        out_shape=(jax.ShapeDtypeStruct((HALF, F), F32), mat, mat),
        in_specs=[ANY],
        out_specs=(VMEM, VMEM, VMEM),
        scratch_shapes=[
            pltpu.VMEM((2 * F, F), F32),
            pltpu.VMEM((2 * F, F), F32),
            pltpu.VMEM((F, F), F32),
            pltpu.SemaphoreType.DMA((2,)),
        ]
        + INVERT_SCRATCH,
        compiler_params=params(56),
        cost_estimate=pl.CostEstimate(flops=40 * 10**9, transcendentals=0, bytes_accessed=12 * 10**6),
        name="level_one",
    )(g)


def between_body(g, t, si, keep, m_out, base_out, a_out, c_ref, sems):
    gc = pltpu.make_async_copy(g.at[1], c_ref, sems.at[0])
    gc.start()
    gc.wait()
    i = (lax.axis_index("zl") * 2 + lax.axis_index("core")) * ROWS
    i = pl.multiple_of(i, ROWS)
    low = lax.axis_index("xl") == 0
    tt = split2(t[...])
    sis = split2(si[...])
    ca = split2(c_ref[:F, :])
    cb = split2(c_ref[F:, :])

    @pl.when(low)
    def _():
        rows = split2(c_ref[pl.ds(i, ROWS), :])
        y = mul3(rows, sis, NN)
        base_out[...] = keep[...] - mul3(split2(y), ca, NT)
        a_out[...] = -mul3(rows, tt, NN)
        m_out[...] = -mul3(tt, ca, TT)

    @pl.when(jnp.logical_not(low))
    def _():
        r_ = lax.broadcasted_iota(jnp.int32, (ROWS, F), 0) + i
        c_ = lax.broadcasted_iota(jnp.int32, (ROWS, F), 1)
        e = jnp.where(r_ == c_, 1.0, 0.0).astype(BF16)
        rows = (dg(e, cb[0], NT).astype(BF16), dg(e, cb[1], NT).astype(BF16))
        y = mul3(rows, sis, NN)
        base_out[...] = keep[...] - mul3(split2(y), cb, NN)
        a_out[...] = -mul3(rows, tt, NT)
        m_out[...] = -mul3(tt, cb, NN)


def between(g, t, si, keep):
    rows = jax.ShapeDtypeStruct((ROWS, F), F32)
    return pl.pallas_call(
        between_body,
        out_shape=(jax.ShapeDtypeStruct((F, F), F32), rows, rows),
        in_specs=[ANY, VMEM, VMEM, VMEM],
        out_specs=(VMEM, VMEM, VMEM),
        scratch_shapes=[pltpu.VMEM((2 * F, F), F32), pltpu.SemaphoreType.DMA((1,))],
        compiler_params=params(56),
        cost_estimate=pl.CostEstimate(flops=6 * 10**9, transcendentals=0, bytes_accessed=12 * 10**6),
        name="between",
    )(g, t, si, keep)


def level_two_body(q, mine, theirs, m, base, a, b, ro, out, m_ref, q_ref, sems, s_ref, *work):
    gq = pltpu.make_async_copy(q, q_ref, sems.at[0])
    gm = pltpu.make_async_copy(m, m_ref, sems.at[1])
    gq.start()
    gm.start()
    gq.wait()
    core = lax.axis_index("core")
    for k in range(16):
        for z in range(2):
            s_ref[48 * k + 24 * z : 48 * k + 24 * z + 24, :] = q_ref[z, k]
    h = pl.multiple_of(core * HALF, HALF)
    o = pl.multiple_of((1 - core) * HALF, HALF)
    s_ref[pl.ds(h, HALF), :] = s_ref[pl.ds(h, HALF), :] - mine[...]
    s_ref[pl.ds(o, HALF), :] = s_ref[pl.ds(o, HALF), :] - theirs[...]
    invert(s_ref, *work)
    gm.wait()
    low = lax.axis_index("xl") == 0
    x = jnp.concatenate([jnp.where(low, a[...], b[...]), a[...]], axis=0)
    y = mul3(split2(x), split2(s_ref[:F, :]), NN)
    z = mul3(split2(y), split2(m_ref[...]), NN)
    first = jnp.where(low, base[...], 0.0) - z[:ROWS]
    second = base[...] - z[ROWS:]
    p = onehot_of(ro[...])
    out[...] = pick(jnp.concatenate([first, second], axis=0), p, NT)


def level_two(q, mine, theirs, m, base, a, b, ro):
    return pl.pallas_call(
        level_two_body,
        out_shape=jax.ShapeDtypeStruct((2 * ROWS, F), F32),
        in_specs=[ANY, VMEM, VMEM, ANY, VMEM, VMEM, VMEM, VMEM],
        out_specs=VMEM,
        scratch_shapes=[
            pltpu.VMEM((F, F), F32),
            pltpu.VMEM((2, 16, 24, F), F32),
            pltpu.SemaphoreType.DMA((2,)),
        ]
        + INVERT_SCRATCH,
        compiler_params=params(56),
        cost_estimate=pl.CostEstimate(flops=40 * 10**9, transcendentals=0, bytes_accessed=12 * 10**6),
        name="level_two",
    )(q, mine, theirs, m, base, a, b, ro)


def shards(row_owner, face_left, face_cross, face_right):
    ro = row_owner.reshape(1, F)
    zh = lax.axis_index("zh")
    xl = lax.axis_index("xl")
    send, other = enter(ro, face_left[0, 0], face_cross[0, 0], face_right[0, 0])
    g = lax.all_gather(send, PAIR, axis=1, tiled=True)
    partner = lax.ppermute(other, "zh", SWAP)
    own = zh == xl
    keep = jnp.where(own, other, partner)
    give = jnp.where(own, partner, other)
    q = give + lax.ppermute(give, "xl", SWAP)
    q = lax.dynamic_slice_in_dim(q, zh * 24, 24, 0)
    q = lax.all_gather(q, PAIR, axis=0, tiled=True).reshape(2, 16, 24, F)
    v, t, si = level_one(g)
    v2 = lax.ppermute(v, "xl", SWAP)
    m, base, a = between(g, t, si, keep)
    b = lax.ppermute(a, "xl", SWAP)
    v2, m, base, a, b = lax.optimization_barrier((v2, m, base, a, b))
    w = v + v2
    w2 = lax.ppermute(w, "core", SWAP)
    mine = level_two(q, w, w2, m, base, a, b, ro)
    theirs = lax.ppermute(mine, "xl", SWAP)
    low = xl == 0
    left = jnp.where(low, mine[:ROWS], theirs[:ROWS])
    cross = jnp.where(low, theirs[:ROWS], mine[:ROWS])
    right = jnp.where(low, theirs[ROWS:], mine[ROWS:])
    return (left[None, None], cross[None, None], right[None, None])


def solution(mesh):
    fine = Mesh(mesh.devices.reshape(8, 2, 4, 2, 2, 2), ("zl", "core", "y", "zh", "xh", "xl"))
    face = P(("y", "zh"), ("xh", "xl"), ("zl", "core"), None)
    return jax.shard_map(
        shards, mesh=fine, in_specs=(P(), face, face, face), out_specs=(face, face, face), check_vma=False
    )
```

time: 842 us -> 240 us (0.29)
  other arithmetic: 386 us -> 3.24 us
  waiting for transfers between devices: 269 us -> 90.3 us
  Pallas kernels: 0 us -> 95.1 us
  local copies, waits for them, and re-layouts: 71.9 us -> 4.45 us
  matrix products: 66.5 us -> 0 us
  starting transfers between devices: 19.1 us -> 31.4 us
  between operations: 23.6 us -> 14.2 us
    another operation x56 -> x0, other arithmetic: 378 us -> none  [the longest x46 249 us: shards(): factor = jnp.linalg.cholesky(gathered[0])]
    all_gather x2, waiting for transfers between devices: 248 us -> 58.7 us  [the longest x1 58.7 us: shards(): g = lax.all_gather(send, PAIR, axis=1, tiled=True)]
    pallas_call x0 -> x4, Pallas kernels: none -> 95.1 us  [the longest x1 41.5 us: level_one(): pl.pallas_call(level_one_body, out_shape=(jax.ShapeDtypeStruct((HALF, F),...]
    another operation x108 -> x0, matrix products: 52.3 us -> none  [the longest x44 22 us: merge_rows(): weights = jax.scipy.linalg.cho_solve((factor, True), columns)]
    another operation x61 -> x0, local copies, waits for them, and re-layouts: 37.6 us -> none  [the longest x43 35.8 us: merge_rows(): solved = jax.scipy.linalg.cho_solve((factor, True), first[1].T).T]
    dot_general x6 -> x0, matrix products: 14.2 us -> none  [the longest x2 6.39 us: dot_against(): lax.dot_general(left, right, (((1,), (1,)), ((), ())), precision=lax.Prec...]
    ppermute x2 -> x6, starting transfers between devices: 19 us -> 31.4 us  [the longest x1 15.7 us: shards(): partner = lax.ppermute(other, 'zh', SWAP)]
    unnamed x65 -> x16, local copies, waits for them, and re-layouts: 13.7 us -> 3.76 us
  transfers between devices with their start and end apart: 4 -> 8, of which waited for: 4 -> 6; matrix products, arithmetic and copies ran while one was open for 0% -> 1% of each run, Pallas kernels for 0% -> 23%
where the time goes in v1:
time: 240 us; the launch traced here: 239 us
  Pallas kernels  95.1 us (40%)
  waiting for transfers between devices  90.3 us (38%)
  starting transfers between devices  31.4 us (13%)
  between operations  14.2 us (6%)
  local copies, waits for them, and re-layouts  4.45 us (2%)
  other arithmetic  3.24 us (1%)
    all_gather x1, waiting for transfers between devices, shards(): g = lax.all_gather(send, PAIR, axis=1, tiled=True)  58.7 us
    pallas_call x1, Pallas kernels, level_one(): pl.pallas_call(level_one_body, out_shape=(jax.ShapeDtypeStruct((HALF, F),...  41.5 us
    pallas_call x1, Pallas kernels, level_two(): pl.pallas_call(level_two_body, out_shape=jax.ShapeDtypeStruct((2 * ROWS,...  37.2 us
    ppermute x1, starting transfers between devices, shards(): partner = lax.ppermute(other, 'zh', SWAP)  15.7 us
    pallas_call x1, Pallas kernels, between(): pl.pallas_call(between_body, out_shape=(jax.ShapeDtypeStruct((F, F), F32)...  13.7 us
    ppermute x1, waiting for transfers between devices, shards(): b = lax.ppermute(a, 'xl', SWAP)  13.5 us
    ppermute x1, waiting for transfers between devices, shards(): theirs = lax.ppermute(mine, 'xl', SWAP)  7.5 us
  transfers between devices with their start and end apart: 8, of which 6 were waited for; matrix products, arithmetic and copies ran while one was open for 1% of the time, Pallas kernels for 23%

profile of v1, /device:TPU:24, one launch (start us, length us, event | category | flops | bytes accessed | tf_op | source)
XLA Modules:
  0.0 238.6 jit_solution(17924194266517431322)
XLA Ops:
  7.2 0.0 all-gather.5.cloned.1.call-start
  7.2 0.7 reshape.12.ro
  7.9 0.0 copy-start.3
  7.9 0.0 copy-start
  7.9 0.9 copy-done
  8.8 0.0 copy-start.1
  8.8 0.9 copy-done.1
  9.7 0.0 copy-start.2
  9.7 0.9 copy-done.2
  10.6 2.7 %enter.1 = (f32[2,48,768]{2,1,0:T(8,128)}, f32[48,768]{1,0:T(8,128)S(1)}) custom-call(s32[1,768]{1,0:T(1,128)S(1)} %reshape.12.ro, f32[48,768]{1,0:T(8,128)S(1)} %bitcast.10, f32[48,768]{1,0:T(8,128)S(1)} %bitcast.11, f32[48,768]{1,0:T(8,128)S(1)} %bitcast.12), custom_call_target="tpu_custom_call" | custom-call | tf_op jit(solution)/shard_map/enter/pallas_call | solution.py:194
  13.3 0.0 all-gather.5.cloned.1.call-update
  13.3 0.0 all-gather.3.cloned.1.call-start
  13.4 15.7 %collective-permute-start = (f32[48,768]{1,0:T(8,128)S(1)}, f32[48,768]{1,0:T(8,128)S(1)}, u32[]{:S(2)}, u32[]{:S(2)}) collective-permute-start(f32[48,768]{1,0:T(8,128)S(1)} %get-tuple-element.16), channel_id=1, source_target_pairs={{0,4},{4,0},{1,5},{5,1},{2,6},{6,2},{3,7},{7,3},{8,12},{12,8},{9,1... | collective-permute-start | bytes 442376 | tf_op jit(solution)/shard_map/ppermute | solution.py:351
  29.1 4.1 %collective-permute-done = f32[48,768]{1,0:T(8,128)S(1)} collective-permute-done((f32[48,768]{1,0:T(8,128)S(1)}, f32[48,768]{1,0:T(8,128)S(1)}, u32[]{:S(2)}, u32[]{:S(2)}) %collective-permute-start) | collective-permute-done | bytes 147488 | tf_op jit(solution)/shard_map/ppermute | solution.py:351
  33.3 0.7 broadcast_select_fusion
  33.9 3.4 %collective-permute-start.1 = (f32[48,768]{1,0:T(8,128)S(1)}, f32[48,768]{1,0:T(8,128)S(1)}, u32[]{:S(2)}, u32[]{:S(2)}) collective-permute-start(f32[48,768]{1,0:T(8,128)S(1)} %get-tuple-element.33), channel_id=1, source_target_pairs={{0,1},{1,0},{2,3},{3,2},{4,5},{5,4},{6,7},{7,6},{8,9},{9,8},{10,11... | collective-permute-start | bytes 442376 | tf_op jit(solution)/shard_map/ppermute | solution.py:355
  37.3 3.6 %collective-permute-done.1 = f32[48,768]{1,0:T(8,128)S(1)} collective-permute-done((f32[48,768]{1,0:T(8,128)S(1)}, f32[48,768]{1,0:T(8,128)S(1)}, u32[]{:S(2)}, u32[]{:S(2)}) %collective-permute-start.1) | collective-permute-done | bytes 147488 | tf_op jit(solution)/shard_map/ppermute | solution.py:355
  41.0 0.6 dynamic-slice_add_fusion
  41.6 0.0 all-gather.3.cloned.1.call-update
  41.6 58.7 %all-gather.5.cloned.1.call-done.g = f32[2,1536,768]{2,1,0:T(8,128)} async-done(((f32[2,48,768]{2,1,0:T(8,128)}), f32[2,1536,768]{2,1,0:T(8,128)}) %all-gather.5.cloned.1.call-update) | async-done | bytes 9437200 | tf_op jit(solution)/shard_map/all_gather | solution.py:350
  100.3 41.5 %level_one.1 = (f32[384,768]{1,0:T(8,128)}, f32[768,768]{1,0:T(8,128)}, f32[768,768]{1,0:T(8,128)}) custom-call(f32[2,1536,768]{2,1,0:T(8,128)} %all-gather.5.cloned.1.call-done.g), custom_call_target="tpu_custom_call" | custom-call | flops 40000000000 | bytes 12000000 | tf_op jit(solution)/shard_map/level_one/pallas_call | solution.py:237
  141.8 0.0 copy-done.3
  141.8 4.1 %collective-permute-start.2 = (f32[384,768]{1,0:T(8,128)}, f32[384,768]{1,0:T(8,128)S(1)}, u32[]{:S(2)}, u32[]{:S(2)}) collective-permute-start(f32[384,768]{1,0:T(8,128)} %get-tuple-element.18), channel_id=1, source_target_pairs={{0,1},{1,0},{2,3},{3,2},{4,5},{5,4},{6,7},{7,6},{8,9},{9,8},{10,11... | collective-permute-start | bytes 3538952 | tf_op jit(solution)/shard_map/ppermute | solution.py:359
  146.0 0.0 copy-start.4
  146.0 13.7 %between.1 = (f32[768,768]{1,0:T(8,128)}, f32[48,768]{1,0:T(8,128)}, f32[48,768]{1,0:T(8,128)}) custom-call(f32[2,1536,768]{2,1,0:T(8,128)} %all-gather.5.cloned.1.call-done.g, f32[768,768]{1,0:T(8,128)} %get-tuple-element.19.t, f32[768,768]{1,0:T(8,128)} %get-tuple-element.20.si, f32[48,768]{1,0:T(8,128)} %get-tuple-element.32.keep), custom_call_target="tpu_custom_call" | custom-call | flops 6000000000 | bytes 12000000 | tf_op jit(solution)/shard_map/between/pallas_call | solution.py:289
  159.6 2.6 %collective-permute-start.3 = (f32[48,768]{1,0:T(8,128)}, f32[48,768]{1,0:T(8,128)S(1)}, u32[]{:S(2)}, u32[]{:S(2)}) collective-permute-start(f32[48,768]{1,0:T(8,128)} %get-tuple-element.27.a), channel_id=1, source_target_pairs={{0,1},{1,0},{2,3},{3,2},{4,5},{5,4},{6,7},{7,6},{8,9},{9,8},{10,11... | collective-permute-start | bytes 442376 | tf_op jit(solution)/shard_map/ppermute | solution.py:361
  162.2 13.5 %collective-permute-done.3.b = f32[48,768]{1,0:T(8,128)S(1)} collective-permute-done((f32[48,768]{1,0:T(8,128)}, f32[48,768]{1,0:T(8,128)S(1)}, u32[]{:S(2)}, u32[]{:S(2)}) %collective-permute-start.3) | collective-permute-done | bytes 147488 | tf_op jit(solution)/shard_map/ppermute | solution.py:361
  175.7 0.0 copy-start.7
  175.7 0.0 collective-permute-done.2
  175.7 0.0 copy-done.4
  175.7 0.1 add.11.mine
  175.8 0.0 copy-start.5
  175.9 1.9 collective-permute-start.4
  177.8 0.0 all-gather.3.cloned.1.call-done
  177.8 2.8 %collective-permute-done.4.theirs = f32[384,768]{1,0:T(8,128)S(1)} collective-permute-done((f32[384,768]{1,0:T(8,128)S(1)}, f32[384,768]{1,0:T(8,128)S(1)}, u32[]{:S(2)}, u32[]{:S(2)}) %collective-permute-start.4) | collective-permute-done | bytes 1179680 | tf_op jit(solution)/shard_map/ppermute | solution.py:364
  180.6 0.0 copy-start.6
  180.6 0.0 copy-done.7
  180.6 0.0 copy-done.5
  180.6 1.0 copy-done.6
  181.6 37.2 %level_two.1 = f32[96,768]{1,0:T(8,128)} custom-call(f32[2,16,24,768]{3,2,1,0:T(8,128)} %bitcast.13, f32[384,768]{1,0:T(8,128)} %copy-done.5, f32[384,768]{1,0:T(8,128)} %copy-done.6, f32[768,768]{1,0:T(8,128)} %get-tuple-element.25.m, f32[48,768]{1,0:T(8,128)} %get-tuple-element.26.base, f32[48,768]{1,0:T(8,128)} %get-tuple-element.27.a, ...), custom_call_target="tpu_custom_call" | custom-call | flops 40000000000 | bytes 12000000 | tf_op jit(solution)/shard_map/level_two/pallas_call | solution.py:328
  218.9 3.6 %collective-permute-start.5 = (f32[96,768]{1,0:T(8,128)}, f32[96,768]{1,0:T(8,128)S(1)}, u32[]{:S(2)}, u32[]{:S(2)}) collective-permute-start(f32[96,768]{1,0:T(8,128)} %level_two.1), channel_id=1, source_target_pairs={{0,1},{1,0},{2,3},{3,2},{4,5},{5,4},{6,7},{7,6},{8,9},{9,8},{10,11... | collective-permute-start | bytes 884744 | tf_op jit(solution)/shard_map/ppermute | solution.py:366
  222.5 7.5 %collective-permute-done.5 = f32[96,768]{1,0:T(8,128)S(1)} collective-permute-done((f32[96,768]{1,0:T(8,128)}, f32[96,768]{1,0:T(8,128)S(1)}, u32[]{:S(2)}, u32[]{:S(2)}) %collective-permute-start.5) | collective-permute-done | bytes 294944 | tf_op jit(solution)/shard_map/ppermute | solution.py:366
  230.0 1.8 fusion
Async XLA Ops:
  7.2 93.2 %all-gather.5.cloned.1.call-start = ((), (), s32[]{:S(2)}) async-start(), calls=%async_computation.1 | async-start | bytes 9732096 | tf_op jit(solution)/shard_map/all_gather | solution.py:350
  7.9 133.9 %copy-start.3 = (s32[1,768]{1,0:T(1,128)}, s32[1,768]{1,0:T(1,128)S(1)}, u32[]{:S(2)}) copy-start(s32[1,768]{1,0:T(1,128)S(1)} %reshape.12.ro) | copy-start | bytes 9220
  7.9 0.9 copy-start
  8.8 0.9 copy-start.1
  9.7 0.9 copy-start.2
  13.3 164.5 %all-gather.3.cloned.1.call-start = ((), (), s32[]{:S(2)}) async-start(), calls=%async_computation | async-start | bytes 2433024 | tf_op jit(solution)/shard_map/all_gather | solution.py:357
  13.4 19.9 %collective-permute-start = (f32[48,768]{1,0:T(8,128)S(1)}, f32[48,768]{1,0:T(8,128)S(1)}, u32[]{:S(2)}, u32[]{:S(2)}) collective-permute-start(f32[48,768]{1,0:T(8,128)S(1)} %get-tuple-element.16), channel_id=1, source_target_pairs={{0,4},{4,0},{1,5},{5,1},{2,6},{6,2},{3,7},{7,3},{8,12},{12,8},{9,1... | collective-permute-start | bytes 442376 | tf_op jit(solution)/shard_map/ppermute | solution.py:351
  33.9 7.0 %collective-permute-start.1 = (f32[48,768]{1,0:T(8,128)S(1)}, f32[48,768]{1,0:T(8,128)S(1)}, u32[]{:S(2)}, u32[]{:S(2)}) collective-permute-start(f32[48,768]{1,0:T(8,128)S(1)} %get-tuple-element.33), channel_id=1, source_target_pairs={{0,1},{1,0},{2,3},{3,2},{4,5},{5,4},{6,7},{7,6},{8,9},{9,8},{10,11... | collective-permute-start | bytes 442376 | tf_op jit(solution)/shard_map/ppermute | solution.py:355
  141.8 33.9 %collective-permute-start.2 = (f32[384,768]{1,0:T(8,128)}, f32[384,768]{1,0:T(8,128)S(1)}, u32[]{:S(2)}, u32[]{:S(2)}) collective-permute-start(f32[384,768]{1,0:T(8,128)} %get-tuple-element.18), channel_id=1, source_target_pairs={{0,1},{1,0},{2,3},{3,2},{4,5},{5,4},{6,7},{7,6},{8,9},{9,8},{10,11... | collective-permute-start | bytes 3538952 | tf_op jit(solution)/shard_map/ppermute | solution.py:359
  146.0 29.7 %copy-start.4 = (f32[384,768]{1,0:T(8,128)S(1)}, f32[384,768]{1,0:T(8,128)}, u32[]{:S(2)}) copy-start(f32[384,768]{1,0:T(8,128)} %get-tuple-element.18) | copy-start | bytes 3538948
  159.6 16.0 %collective-permute-start.3 = (f32[48,768]{1,0:T(8,128)}, f32[48,768]{1,0:T(8,128)S(1)}, u32[]{:S(2)}, u32[]{:S(2)}) collective-permute-start(f32[48,768]{1,0:T(8,128)} %get-tuple-element.27.a), channel_id=1, source_target_pairs={{0,1},{1,0},{2,3},{3,2},{4,5},{5,4},{6,7},{7,6},{8,9},{9,8},{10,11... | collective-permute-start | bytes 442376 | tf_op jit(solution)/shard_map/ppermute | solution.py:361
  175.7 4.9 %copy-start.7 = (f32[48,768]{1,0:T(8,128)}, f32[48,768]{1,0:T(8,128)S(1)}, u32[]{:S(2)}) copy-start(f32[48,768]{1,0:T(8,128)S(1)} %collective-permute-done.3.b) | copy-start | bytes 442372
  175.8 4.8 %copy-start.5 = (f32[384,768]{1,0:T(8,128)}, f32[384,768]{1,0:T(8,128)S(1)}, u32[]{:S(2)}) copy-start(f32[384,768]{1,0:T(8,128)S(1)} %add.11.mine) | copy-start | bytes 3538948
  175.9 4.7 %collective-permute-start.4 = (f32[384,768]{1,0:T(8,128)S(1)}, f32[384,768]{1,0:T(8,128)S(1)}, u32[]{:S(2)}, u32[]{:S(2)}) collective-permute-start(f32[384,768]{1,0:T(8,128)S(1)} %add.11.mine), channel_id=1, source_target_pairs={{0,32},{32,0},{1,33},{33,1},{2,34},{34,2},{3,35},{35,3},{4,36},{36... | collective-permute-start | bytes 3538952 | tf_op jit(solution)/shard_map/ppermute | solution.py:364
  180.6 1.0 copy-start.6
  218.9 11.2 %collective-permute-start.5 = (f32[96,768]{1,0:T(8,128)}, f32[96,768]{1,0:T(8,128)S(1)}, u32[]{:S(2)}, u32[]{:S(2)}) collective-permute-start(f32[96,768]{1,0:T(8,128)} %level_two.1), channel_id=1, source_target_pairs={{0,1},{1,0},{2,3},{3,2},{4,5},{5,4},{6,7},{7,6},{8,9},{9,8},{10,11... | collective-permute-start | bytes 884744 | tf_op jit(solution)/shard_map/ppermute | solution.py:366
Sparse Core Ops, SparseCore 0:
  13.5 86.8 all-gather.4
  102.4 67.7 all-gather.2

commit v2 on v1

--- a/solution.py
+++ b/solution.py
@@ -10,7 +10,6 @@
 
 F = 768
 ROWS = 48
-HALF = 384
 B = 128
 F32 = jnp.float32
 BF16 = jnp.bfloat16
@@ -48,6 +47,22 @@
 
 def mul3(a, b, dims):
     return (dg(a[1], b[0], dims) + dg(a[0], b[1], dims)) + dg(a[0], b[0], dims)
+
+
+def mul6full(a, b):
+    low = (dg(a[2], b[0], NN) + dg(a[0], b[2], NN)) + dg(a[1], b[1], NN)
+    return (low + (dg(a[1], b[0], NN) + dg(a[0], b[1], NN))) + dg(a[0], b[0], NN)
+
+
+def mul_into(out_ref, x_ref, y_ref, xh_ref, xl_ref):
+    xh_ref[...], xl_ref[...] = split2(x_ref[...])
+
+    def tile(j, carry):
+        js = pl.ds(pl.multiple_of(j * 256, 256), 256)
+        out_ref[:, js] = mul3((xh_ref[...], xl_ref[...]), split2(y_ref[:, js]), NN)
+        return carry
+
+    lax.fori_loop(0, F // 256, tile, 0)
 
 
 def pick(x, onehot, dims):
@@ -181,13 +196,13 @@
 ]
 
 
-def enter_body(ro, left, cross, right, send, other):
+def enter_body(ro, left, cross, right, send, part):
     p = onehot_of(ro[...])
     upper = lax.axis_index("zh") == 1
     l, c, r = left[...], cross[...], right[...]
-    send[0] = pick(jnp.where(upper, l, r), p, NN)
-    send[1] = pick(c, p, NN)
-    other[...] = pick(jnp.where(upper, r, l), p, NN)
+    part[...] = pick(jnp.where(upper, l, r), p, NN)
+    send[0] = pick(c, p, NN)
+    send[1] = pick(jnp.where(upper, r, l), p, NN)
 
 
 def enter(ro, left, cross, right):
@@ -201,168 +216,243 @@
     )(ro, left, cross, right)
 
 
-def level_one_body(g, v_out, t_out, si_out, a_ref, c_ref, t_ref, sems, s_ref, *work):
-    ga = pltpu.make_async_copy(g.at[0], a_ref, sems.at[0])
-    gc = pltpu.make_async_copy(g.at[1], c_ref, sems.at[1])
-    ga.start()
-    gc.start()
-    ga.wait()
-    s_ref[:F, :] = a_ref[:F, :] + a_ref[F:, :]
+def level_one_body(mine, theirs, si_out, s_ref, *work):
+    core = lax.axis_index("core")
+    zl = lax.axis_index("zl")
+    for k in range(8):
+        at = lax.rem(zl + k, 8) * (2 * ROWS)
+        s_ref[pl.ds(pl.multiple_of(at + core * ROWS, ROWS), ROWS), :] = mine[ROWS * k : ROWS * k + ROWS, :]
+        s_ref[pl.ds(pl.multiple_of(at + (1 - core) * ROWS, ROWS), ROWS), :] = theirs[ROWS * k : ROWS * k + ROWS, :]
     invert(s_ref, *work)
-    gc.wait()
     si_out[...] = s_ref[:F, :]
-    si = split2(s_ref[:F, :])
-    h = pl.multiple_of(lax.axis_index("core") * HALF, HALF)
-    low = lax.axis_index("xl") == 0
-
-    @pl.when(low)
-    def _():
-        cb = split2(c_ref[F:, :])
-        t = mul3(si, cb, NN)
-        t_out[...] = t
-        part = split2(c_ref[F:, pl.ds(h, HALF)])
-        v_out[...] = mul3(part, split2(t), TN)
-
-    @pl.when(jnp.logical_not(low))
-    def _():
-        ca = split2(c_ref[:F, :])
-        t_ref[...] = mul3(ca, si, NN)
-        t_out[...] = t_ref[...]
-        part = split2(t_ref[pl.ds(h, HALF), :])
-        v_out[...] = mul3(part, ca, NT)
-
-
-def level_one(g):
-    mat = jax.ShapeDtypeStruct((F, F), F32)
+
+
+def level_one(mine, theirs):
     return pl.pallas_call(
         level_one_body,
-        out_shape=(jax.ShapeDtypeStruct((HALF, F), F32), mat, mat),
-        in_specs=[ANY],
-        out_specs=(VMEM, VMEM, VMEM),
-        scratch_shapes=[
-            pltpu.VMEM((2 * F, F), F32),
-            pltpu.VMEM((2 * F, F), F32),
-            pltpu.VMEM((F, F), F32),
-            pltpu.SemaphoreType.DMA((2,)),
-        ]
-        + INVERT_SCRATCH,
+        out_shape=jax.ShapeDtypeStruct((F, F), F32),
+        in_specs=[VMEM, VMEM],
+        out_specs=VMEM,
+        scratch_shapes=INVERT_SCRATCH,
+        compiler_params=params(40),
+        cost_estimate=pl.CostEstimate(flops=40 * 10**9, transcendentals=0, bytes_accessed=5 * 10**6),
+        name="level_one",
+    )(mine, theirs)
+
+
+def products_body(si, g, w_out, t_out, x_ref, y_ref, o_ref, t_ref, xh_ref, xl_ref, sems):
+    low = lax.axis_index("xl") == 0
+    first = lax.axis_index("core") == 0
+    go = pltpu.make_async_copy(g.at[1, pl.ds(pl.multiple_of(jnp.where(low, F, 0), F), F)], o_ref, sems.at[2])
+
+    @pl.when(low)
+    def _():
+        pltpu.make_async_copy(si, x_ref, sems.at[0]).start()
+        pltpu.make_async_copy(g.at[0, F:], y_ref, sems.at[1]).start()
+
+    @pl.when(jnp.logical_not(low))
+    def _():
+        pltpu.make_async_copy(g.at[0, :F], x_ref, sems.at[0]).start()
+        pltpu.make_async_copy(si, y_ref, sems.at[1]).start()
+
+    go.start()
+    pltpu.make_async_copy(si, x_ref, sems.at[0]).wait()
+    pltpu.make_async_copy(si, y_ref, sems.at[1]).wait()
+    mul_into(t_ref, x_ref, y_ref, xh_ref, xl_ref)
+    out = pltpu.make_async_copy(t_ref, t_out, sems.at[0])
+    out.start()
+    go.wait()
+
+    def panels(block):
+        @pl.when(first)
+        def _():
+            w_out[:, :768] = o_ref[:B, :] - block(0)
+            w_out[:, 768:] = o_ref[B : 2 * B, B:] - block(1)
+
+        @pl.when(jnp.logical_not(first))
+        def _():
+            w_out[:, :512] = o_ref[2 * B : 3 * B, 2 * B :] - block(2)
+            w_out[:, 512:896] = o_ref[3 * B : 4 * B, 3 * B :] - block(3)
+            w_out[:, 896:1152] = o_ref[4 * B : 5 * B, 4 * B :] - block(4)
+            w_out[:, 1152:1280] = o_ref[5 * B :, 5 * B :] - block(5)
+            w_out[:, 1280:] = jnp.zeros((B, B), F32)
+
+    @pl.when(low)
+    def _():
+        panels(lambda i: mul3(split2(y_ref[:, B * i : B * i + B]), split2(t_ref[:, B * i :]), TN))
+
+    @pl.when(jnp.logical_not(low))
+    def _():
+        panels(
+            lambda i: mul3(split2(t_ref[B * i : B * i + B, :]), (xh_ref[B * i :, :], xl_ref[B * i :, :]), NT)
+        )
+
+    out.wait()
+
+
+def products(si, g):
+    return pl.pallas_call(
+        products_body,
+        out_shape=(jax.ShapeDtypeStruct((B, 11 * B), F32), jax.ShapeDtypeStruct((F, F), F32)),
+        in_specs=[ANY, ANY],
+        out_specs=(VMEM, ANY),
+        scratch_shapes=[pltpu.VMEM((F, F), F32)] * 4
+        + [pltpu.VMEM((F, F), BF16)] * 2
+        + [pltpu.SemaphoreType.DMA((3,))],
         compiler_params=params(56),
-        cost_estimate=pl.CostEstimate(flops=40 * 10**9, transcendentals=0, bytes_accessed=12 * 10**6),
-        name="level_one",
-    )(g)
-
-
-def between_body(g, t, si, keep, m_out, base_out, a_out, c_ref, sems):
-    gc = pltpu.make_async_copy(g.at[1], c_ref, sems.at[0])
-    gc.start()
-    gc.wait()
+        cost_estimate=pl.CostEstimate(flops=6 * 10**9, transcendentals=0, bytes_accessed=12 * 10**6),
+        name="products",
+    )(si, g)
+
+
+def between_body(g, t, si, m_out, base_out, a_out, x_ref, y_ref, s_ref, m_ref, xh_ref, xl_ref, keep, sems):
+    low = lax.axis_index("xl") == 0
     i = (lax.axis_index("zl") * 2 + lax.axis_index("core")) * ROWS
     i = pl.multiple_of(i, ROWS)
-    low = lax.axis_index("xl") == 0
-    tt = split2(t[...])
-    sis = split2(si[...])
-    ca = split2(c_ref[:F, :])
-    cb = split2(c_ref[F:, :])
+    gk = pltpu.make_async_copy(
+        g.at[1, pl.ds(pl.multiple_of(i + jnp.where(low, 0, F), ROWS), ROWS)], keep, sems.at[2]
+    )
+    gs = pltpu.make_async_copy(si, s_ref, sems.at[3])
 
     @pl.when(low)
     def _():
-        rows = split2(c_ref[pl.ds(i, ROWS), :])
-        y = mul3(rows, sis, NN)
-        base_out[...] = keep[...] - mul3(split2(y), ca, NT)
-        a_out[...] = -mul3(rows, tt, NN)
-        m_out[...] = -mul3(tt, ca, TT)
+        pltpu.make_async_copy(g.at[0, :F], x_ref, sems.at[0]).start()
+        pltpu.make_async_copy(t, y_ref, sems.at[1]).start()
+
+    @pl.when(jnp.logical_not(low))
+    def _():
+        pltpu.make_async_copy(t, x_ref, sems.at[0]).start()
+        pltpu.make_async_copy(g.at[0, F:], y_ref, sems.at[1]).start()
+
+    gk.start()
+    gs.start()
+    pltpu.make_async_copy(t, x_ref, sems.at[0]).wait()
+    pltpu.make_async_copy(t, y_ref, sems.at[1]).wait()
+    mul_into(m_ref, x_ref, y_ref, xh_ref, xl_ref)
+    out = pltpu.make_async_copy(m_ref, m_out, sems.at[0])
+    out.start()
+    gk.wait()
+    gs.wait()
+    s = split2(s_ref[...])
+
+    @pl.when(low)
+    def _():
+        rows = (xh_ref[pl.ds(i, ROWS), :], xl_ref[pl.ds(i, ROWS), :])
+        z = mul3(rows, s, NN)
+        base_out[...] = keep[...] - mul3(split2(z), (xh_ref[...], xl_ref[...]), NT)
+        a_out[...] = m_ref[pl.ds(i, ROWS), :]
 
     @pl.when(jnp.logical_not(low))
     def _():
         r_ = lax.broadcasted_iota(jnp.int32, (ROWS, F), 0) + i
         c_ = lax.broadcasted_iota(jnp.int32, (ROWS, F), 1)
         e = jnp.where(r_ == c_, 1.0, 0.0).astype(BF16)
-        rows = (dg(e, cb[0], NT).astype(BF16), dg(e, cb[1], NT).astype(BF16))
-        y = mul3(rows, sis, NN)
-        base_out[...] = keep[...] - mul3(split2(y), cb, NN)
-        a_out[...] = -mul3(rows, tt, NT)
-        m_out[...] = -mul3(tt, cb, NN)
-
-
-def between(g, t, si, keep):
+        y = split2(y_ref[...])
+        rows = (dg(e, y[0], NT).astype(BF16), dg(e, y[1], NT).astype(BF16))
+        z = mul3(rows, s, NN)
+        base_out[...] = keep[...] - mul3(split2(z), y, NN)
+        h, k, l = split3(m_ref[...])
+        a_out[...] = (dg(e, l, NT) + dg(e, k, NT)) + dg(e, h, NT)
+
+    out.wait()
+
+
+def between(g, t, si):
     rows = jax.ShapeDtypeStruct((ROWS, F), F32)
     return pl.pallas_call(
         between_body,
         out_shape=(jax.ShapeDtypeStruct((F, F), F32), rows, rows),
-        in_specs=[ANY, VMEM, VMEM, VMEM],
-        out_specs=(VMEM, VMEM, VMEM),
-        scratch_shapes=[pltpu.VMEM((2 * F, F), F32), pltpu.SemaphoreType.DMA((1,))],
+        in_specs=[ANY, ANY, ANY],
+        out_specs=(ANY, VMEM, VMEM),
+        scratch_shapes=[pltpu.VMEM((F, F), F32)] * 4
+        + [pltpu.VMEM((F, F), BF16)] * 2
+        + [pltpu.VMEM((ROWS, F), F32), pltpu.SemaphoreType.DMA((4,))],
         compiler_params=params(56),
         cost_estimate=pl.CostEstimate(flops=6 * 10**9, transcendentals=0, bytes_accessed=12 * 10**6),
         name="between",
-    )(g, t, si, keep)
-
-
-def level_two_body(q, mine, theirs, m, base, a, b, ro, out, m_ref, q_ref, sems, s_ref, *work):
-    gq = pltpu.make_async_copy(q, q_ref, sems.at[0])
-    gm = pltpu.make_async_copy(m, m_ref, sems.at[1])
-    gq.start()
+    )(g, t, si)
+
+
+def level_two_body(mine, theirs, m, base, a, b, ro, out, m_ref, z_ref, sems, s_ref, *work):
+    gm = pltpu.make_async_copy(m, m_ref, sems.at[0])
     gm.start()
-    gq.wait()
-    core = lax.axis_index("core")
-    for k in range(16):
-        for z in range(2):
-            s_ref[48 * k + 24 * z : 48 * k + 24 * z + 24, :] = q_ref[z, k]
-    h = pl.multiple_of(core * HALF, HALF)
-    o = pl.multiple_of((1 - core) * HALF, HALF)
-    s_ref[pl.ds(h, HALF), :] = s_ref[pl.ds(h, HALF), :] - mine[...]
-    s_ref[pl.ds(o, HALF), :] = s_ref[pl.ds(o, HALF), :] - theirs[...]
+    first = lax.axis_index("core") == 0
+    upper = jnp.where(first, mine[...], theirs[...])
+    lower = jnp.where(first, theirs[...], mine[...])
+    rows = [
+        upper[:, :768],
+        upper[:, 768:],
+        lower[:, :512],
+        lower[:, 512:896],
+        lower[:, 896:1152],
+        lower[:, 1152:1280],
+    ]
+    for i in range(6):
+        s_ref[B * i : B * i + B, B * i :] = rows[i]
+        for j in range(i + 1, 6):
+            s_ref[B * j : B * j + B, B * i : B * i + B] = rows[i][:, B * (j - i) : B * (j - i) + B].T
     invert(s_ref, *work)
     gm.wait()
     low = lax.axis_index("xl") == 0
     x = jnp.concatenate([jnp.where(low, a[...], b[...]), a[...]], axis=0)
-    y = mul3(split2(x), split2(s_ref[:F, :]), NN)
-    z = mul3(split2(y), split2(m_ref[...]), NN)
-    first = jnp.where(low, base[...], 0.0) - z[:ROWS]
-    second = base[...] - z[ROWS:]
+    y = mul6full(split3(x), split3(s_ref[:F, :]))
+    ys = split2(y)
+    ms = split2(m_ref[...])
+
+    @pl.when(low)
+    def _():
+        z_ref[...] = mul3(ys, ms, NT)
+
+    @pl.when(jnp.logical_not(low))
+    def _():
+        z_ref[...] = mul3(ys, ms, NN)
+
+    top = jnp.where(low, base[...], 0.0) - z_ref[:ROWS, :]
+    bottom = base[...] - z_ref[ROWS:, :]
     p = onehot_of(ro[...])
-    out[...] = pick(jnp.concatenate([first, second], axis=0), p, NT)
-
-
-def level_two(q, mine, theirs, m, base, a, b, ro):
+    out[...] = pick(jnp.concatenate([top, bottom], axis=0), p, NT)
+
+
+def level_two(mine, theirs, m, base, a, b, ro):
     return pl.pallas_call(
         level_two_body,
         out_shape=jax.ShapeDtypeStruct((2 * ROWS, F), F32),
-        in_specs=[ANY, VMEM, VMEM, ANY, VMEM, VMEM, VMEM, VMEM],
+        in_specs=[VMEM, VMEM, ANY, VMEM, VMEM, VMEM, VMEM],
         out_specs=VMEM,
-        scratch_shapes=[
-            pltpu.VMEM((F, F), F32),
-            pltpu.VMEM((2, 16, 24, F), F32),
-            pltpu.SemaphoreType.DMA((2,)),
-        ]
+        scratch_shapes=[pltpu.VMEM((F, F), F32), pltpu.VMEM((2 * ROWS, F), F32), pltpu.SemaphoreType.DMA((1,))]
         + INVERT_SCRATCH,
         compiler_params=params(56),
         cost_estimate=pl.CostEstimate(flops=40 * 10**9, transcendentals=0, bytes_accessed=12 * 10**6),
         name="level_two",
-    )(q, mine, theirs, m, base, a, b, ro)
+    )(mine, theirs, m, base, a, b, ro)
+
+
+def shift(x, by):
+    at = lambda z: z % 8 * 2 + z // 8
+    return lax.ppermute(x, ("zl", "zh"), [(at((z + by) % 16), at(z)) for z in range(16)])
 
 
 def shards(row_owner, face_left, face_cross, face_right):
     ro = row_owner.reshape(1, F)
-    zh = lax.axis_index("zh")
     xl = lax.axis_index("xl")
-    send, other = enter(ro, face_left[0, 0], face_cross[0, 0], face_right[0, 0])
+    send, part = enter(ro, face_left[0, 0], face_cross[0, 0], face_right[0, 0])
     g = lax.all_gather(send, PAIR, axis=1, tiled=True)
-    partner = lax.ppermute(other, "zh", SWAP)
-    own = zh == xl
-    keep = jnp.where(own, other, partner)
-    give = jnp.where(own, partner, other)
-    q = give + lax.ppermute(give, "xl", SWAP)
-    q = lax.dynamic_slice_in_dim(q, zh * 24, 24, 0)
-    q = lax.all_gather(q, PAIR, axis=0, tiled=True).reshape(2, 16, 24, F)
-    v, t, si = level_one(g)
-    v2 = lax.ppermute(v, "xl", SWAP)
-    m, base, a = between(g, t, si, keep)
+    mine = part + lax.ppermute(part, "zh", SWAP)
+    ups, downs = [mine], [mine]
+    for _ in range(4):
+        ups.append(shift(ups[-1], 1))
+        if len(downs) < 4:
+            downs.append(shift(downs[-1], -1))
+    pieces = jnp.concatenate(ups + downs[:0:-1], axis=0)
+    si = level_one(pieces, lax.ppermute(pieces, "core", SWAP))
+    w, t = products(si, g)
+    w2 = lax.ppermute(w, "xl", SWAP)
+    m, base, a = between(g, t, si)
     b = lax.ppermute(a, "xl", SWAP)
-    v2, m, base, a, b = lax.optimization_barrier((v2, m, base, a, b))
-    w = v + v2
+    w2, m, base, a, b = lax.optimization_barrier((w2, m, base, a, b))
+    w = w + w2
     w2 = lax.ppermute(w, "core", SWAP)
-    mine = level_two(q, w, w2, m, base, a, b, ro)
+    mine = level_two(w, w2, m, base, a, b, ro)
     theirs = lax.ppermute(mine, "xl", SWAP)
     low = xl == 0
     left = jnp.where(low, mine[:ROWS], theirs[:ROWS])

time: 240 us -> 227 us (0.946)
  waiting for transfers between devices: 90.3 us -> 50.2 us
  starting transfers between devices: 31.4 us -> 67.4 us
  Pallas kernels: 95.1 us -> 86.8 us
    all_gather x1, waiting for transfers between devices: 58.7 us -> 0.01 us  [shards(): g = lax.all_gather(send, PAIR, axis=1, tiled=True)]
    ppermute x3 -> x10, starting transfers between devices: 23.2 us -> 58.5 us  [the longest x7 36.6 us: shift(): lax.ppermute(x, ('zl', 'zh'), [(at((z + by) % 16), at(z)) for z in range(...]
    ppermute x3 -> x10, waiting for transfers between devices: 7.75 us -> 33.6 us  [the longest x7 26.4 us: shift(): lax.ppermute(x, ('zl', 'zh'), [(at((z + by) % 16), at(z)) for z in range(...]
    ppermute x1, waiting for transfers between devices: 13.5 us -> 6.7 us  [shards(): b = lax.ppermute(a, 'xl', SWAP)]
    pallas_call x1, Pallas kernels: 13.7 us -> 9.26 us  [between(): pl.pallas_call(between_body, out_shape=(jax.ShapeDtypeStruct((F, F), F32)...]
    pallas_call x1 -> x2, Pallas kernels: 41.5 us -> 37.6 us  [the longest x1 29.4 us: level_one(): pl.pallas_call(level_one_body, out_shape=jax.ShapeDtypeStruct((F, F), F32...]
    unnamed x16 -> x24, local copies, waits for them, and re-layouts: 3.76 us -> 5.16 us
  transfers between devices with their start and end apart: 8 -> 14, of which waited for: 6 -> 12; matrix products, arithmetic and copies ran while one was open for 1% -> 0% of each run, Pallas kernels for 23% -> 17%
where the time goes in v2:
time: 227 us; the launch traced here: 226 us
  Pallas kernels  86.8 us (38%)
  starting transfers between devices  67.4 us (30%)
  waiting for transfers between devices  50.2 us (22%)
  between operations  14.3 us (6%)
  local copies, waits for them, and re-layouts  5.87 us (3%)
    pallas_call x1, Pallas kernels, level_two(): pl.pallas_call(level_two_body, out_shape=jax.ShapeDtypeStruct((2 * ROWS,...  37.2 us
    ppermute x7, starting transfers between devices, shift(): lax.ppermute(x, ('zl', 'zh'), [(at((z + by) % 16), at(z)) for z in range(...  36.6 us
    pallas_call x1, Pallas kernels, level_one(): pl.pallas_call(level_one_body, out_shape=jax.ShapeDtypeStruct((F, F), F32...  29.4 us
    ppermute x7, waiting for transfers between devices, shift(): lax.ppermute(x, ('zl', 'zh'), [(at((z + by) % 16), at(z)) for z in range(...  26.4 us
    ppermute x1, starting transfers between devices, shards(): mine = part + lax.ppermute(part, 'zh', SWAP)  15.7 us
    pallas_call x1, Pallas kernels, between(): pl.pallas_call(between_body, out_shape=(jax.ShapeDtypeStruct((F, F), F32)...  9.26 us
    pallas_call x1, Pallas kernels, products(): pl.pallas_call(products_body, out_shape=(jax.ShapeDtypeStruct((B, 11 * B)...  8.26 us
    ppermute x1, waiting for transfers between devices, shards(): theirs = lax.ppermute(mine, 'xl', SWAP)  8.02 us
  transfers between devices with their start and end apart: 14, of which 12 were waited for; matrix products, arithmetic and copies ran while one was open for 0% of the time, Pallas kernels for 17%

profile of v2, /device:TPU:24, one launch (start us, length us, event | category | flops | bytes accessed | tf_op | source)
XLA Modules:
  0.0 226.4 jit_solution(5496636272085644106)
XLA Ops:
  7.2 0.0 all-gather.2.cloned.1.call-start
  7.2 0.7 reshape.9.ro
  7.9 0.0 copy-start.3
  7.9 0.0 copy-start
  7.9 0.9 copy-done
  8.8 0.0 copy-start.1
  8.8 0.9 copy-done.1
  9.7 0.0 copy-start.2
  9.7 0.9 copy-done.2
  10.6 2.7 %enter.1 = (f32[2,48,768]{2,1,0:T(8,128)}, f32[48,768]{1,0:T(8,128)S(1)}) custom-call(s32[1,768]{1,0:T(1,128)S(1)} %reshape.9.ro, f32[48,768]{1,0:T(8,128)S(1)} %bitcast.9, f32[48,768]{1,0:T(8,128)S(1)} %bitcast.10, f32[48,768]{1,0:T(8,128)S(1)} %bitcast.11), custom_call_target="tpu_custom_call" | custom-call | tf_op jit(solution)/shard_map/enter/pallas_call | solution.py:209
  13.4 0.0 all-gather.2.cloned.1.call-update
  13.4 15.7 %collective-permute-start = (f32[48,768]{1,0:T(8,128)S(1)}, f32[48,768]{1,0:T(8,128)S(1)}, u32[]{:S(2)}, u32[]{:S(2)}) collective-permute-start(f32[48,768]{1,0:T(8,128)S(1)} %get-tuple-element.15), channel_id=1, source_target_pairs={{0,4},{4,0},{1,5},{5,1},{2,6},{6,2},{3,7},{7,3},{8,12},{12,8},{9,1... | collective-permute-start | bytes 442376 | tf_op jit(solution)/shard_map/ppermute | solution.py:440
  29.1 4.1 %collective-permute-done = f32[48,768]{1,0:T(8,128)S(1)} collective-permute-done((f32[48,768]{1,0:T(8,128)S(1)}, f32[48,768]{1,0:T(8,128)S(1)}, u32[]{:S(2)}, u32[]{:S(2)}) %collective-permute-start) | collective-permute-done | bytes 147488 | tf_op jit(solution)/shard_map/ppermute | solution.py:440
  33.3 12.2 %collective-permute-start.1 = (f32[48,768]{1,0:T(8,128)S(1)}, f32[48,768]{1,0:T(8,128)S(1)}, u32[]{:S(2)}, u32[]{:S(2)}) collective-permute-start(f32[48,768]{1,0:T(8,128)S(1)} %get-tuple-element.28), channel_id=1, source_target_pairs={{64,0},{128,64},{192,128},{256,192},{320,256},{384,320},{448,384},... | collective-permute-start | bytes 442376 | tf_op jit(solution)/shard_map/ppermute | solution.py:432
  45.5 9.3 %collective-permute-done.1 = f32[48,768]{1,0:T(8,128)S(1)} collective-permute-done((f32[48,768]{1,0:T(8,128)S(1)}, f32[48,768]{1,0:T(8,128)S(1)}, u32[]{:S(2)}, u32[]{:S(2)}) %collective-permute-start.1) | collective-permute-done | bytes 147488 | tf_op jit(solution)/shard_map/ppermute | solution.py:432
  54.7 7.5 %collective-permute-start.2 = (f32[48,768]{1,0:T(8,128)S(1)}, f32[48,768]{1,0:T(8,128)S(1)}, u32[]{:S(2)}, u32[]{:S(2)}) collective-permute-start(f32[48,768]{1,0:T(8,128)S(1)} %collective-permute-done.1), channel_id=1, source_target_pairs={{64,0},{128,64},{192,128},{256,192},{320,256},{384,320},{448,384},... | collective-permute-start | bytes 442376 | tf_op jit(solution)/shard_map/ppermute | solution.py:432
  62.2 1.9 collective-permute-start.5
  64.2 3.6 %collective-permute-done.2 = f32[48,768]{1,0:T(8,128)S(1)} collective-permute-done((f32[48,768]{1,0:T(8,128)S(1)}, f32[48,768]{1,0:T(8,128)S(1)}, u32[]{:S(2)}, u32[]{:S(2)}) %collective-permute-start.2) | collective-permute-done | bytes 147488 | tf_op jit(solution)/shard_map/ppermute | solution.py:432
  67.7 5.6 %collective-permute-start.3 = (f32[48,768]{1,0:T(8,128)S(1)}, f32[48,768]{1,0:T(8,128)S(1)}, u32[]{:S(2)}, u32[]{:S(2)}) collective-permute-start(f32[48,768]{1,0:T(8,128)S(1)} %collective-permute-done.2), channel_id=1, source_target_pairs={{64,0},{128,64},{192,128},{256,192},{320,256},{384,320},{448,384},... | collective-permute-start | bytes 442376 | tf_op jit(solution)/shard_map/ppermute | solution.py:432
  73.3 0.3 collective-permute-done.5
  73.7 1.9 collective-permute-start.6
  75.6 3.7 %collective-permute-done.3 = f32[48,768]{1,0:T(8,128)S(1)} collective-permute-done((f32[48,768]{1,0:T(8,128)S(1)}, f32[48,768]{1,0:T(8,128)S(1)}, u32[]{:S(2)}, u32[]{:S(2)}) %collective-permute-start.3) | collective-permute-done | bytes 147488 | tf_op jit(solution)/shard_map/ppermute | solution.py:432
  79.3 5.6 %collective-permute-start.4 = (f32[48,768]{1,0:T(8,128)S(1)}, f32[48,768]{1,0:T(8,128)S(1)}, u32[]{:S(2)}, u32[]{:S(2)}) collective-permute-start(f32[48,768]{1,0:T(8,128)S(1)} %collective-permute-done.3), channel_id=1, source_target_pairs={{64,0},{128,64},{192,128},{256,192},{320,256},{384,320},{448,384},... | collective-permute-start | bytes 442376 | tf_op jit(solution)/shard_map/ppermute | solution.py:432
  85.0 0.2 collective-permute-done.6
  85.1 1.9 collective-permute-start.7
  87.1 3.3 %collective-permute-done.4 = f32[48,768]{1,0:T(8,128)S(1)} collective-permute-done((f32[48,768]{1,0:T(8,128)S(1)}, f32[48,768]{1,0:T(8,128)S(1)}, u32[]{:S(2)}, u32[]{:S(2)}) %collective-permute-start.4) | collective-permute-done | bytes 147488 | tf_op jit(solution)/shard_map/ppermute | solution.py:432
  90.4 0.0 copy-done.3
  90.4 6.0 %collective-permute-done.7 = f32[48,768]{1,0:T(8,128)S(1)} collective-permute-done((f32[48,768]{1,0:T(8,128)S(1)}, f32[48,768]{1,0:T(8,128)S(1)}, u32[]{:S(2)}, u32[]{:S(2)}) %collective-permute-start.7) | collective-permute-done | bytes 147488 | tf_op jit(solution)/shard_map/ppermute | solution.py:432
  96.5 1.9 collective-permute-start.8
  98.4 3.0 %collective-permute-done.8.theirs = f32[384,768]{1,0:T(8,128)S(1)} collective-permute-done((f32[384,768]{1,0:T(8,128)S(1)}, f32[384,768]{1,0:T(8,128)S(1)}, u32[]{:S(2)}, u32[]{:S(2)}) %collective-permute-start.8) | collective-permute-done | bytes 1179680 | tf_op jit(solution)/shard_map/ppermute | solution.py:447
  101.4 29.4 %level_one.1.si = f32[768,768]{1,0:T(8,128)S(1)} custom-call(f32[384,768]{1,0:T(8,128)S(1)} %constant_dynamic-update-slice_fusion.mine, f32[384,768]{1,0:T(8,128)S(1)} %collective-permute-done.8.theirs), custom_call_target="tpu_custom_call" | custom-call | flops 40000000000 | bytes 5000000 | tf_op jit(solution)/shard_map/level_one/pallas_call | solution.py:231
  130.8 0.0 copy-start.4
  130.8 1.4 copy-done.4
  132.2 0.0 all-gather.2.cloned.1.call-done.g
  132.2 8.3 %products.1 = (f32[128,1408]{1,0:T(8,128)}, f32[768,768]{1,0:T(8,128)}) custom-call(f32[768,768]{1,0:T(8,128)} %copy-done.4, f32[2,1536,768]{2,1,0:T(8,128)} %all-gather.2.cloned.1.call-done.g), custom_call_target="tpu_custom_call" | custom-call | flops 6000000000 | bytes 12000000 | tf_op jit(solution)/shard_map/products/pallas_call | solution.py:294
  140.5 4.3 %collective-permute-start.9 = (f32[128,1408]{1,0:T(8,128)}, f32[128,1408]{1,0:T(8,128)S(1)}, u32[]{:S(2)}, u32[]{:S(2)}) collective-permute-start(f32[128,1408]{1,0:T(8,128)} %get-tuple-element.17), channel_id=1, source_target_pairs={{0,1},{1,0},{2,3},{3,2},{4,5},{5,4},{6,7},{7,6},{8,9},{9,8},{10,11... | collective-permute-start | bytes 2162696 | tf_op jit(solution)/shard_map/ppermute | solution.py:449
  144.8 0.0 copy-start.5
  144.8 9.3 %between.1 = (f32[768,768]{1,0:T(8,128)}, f32[48,768]{1,0:T(8,128)}, f32[48,768]{1,0:T(8,128)}) custom-call(f32[2,1536,768]{2,1,0:T(8,128)} %all-gather.2.cloned.1.call-done.g, f32[768,768]{1,0:T(8,128)} %get-tuple-element.18.t, f32[768,768]{1,0:T(8,128)} %copy-done.4), custom_call_target="tpu_custom_call" | custom-call | flops 6000000000 | bytes 12000000 | tf_op jit(solution)/shard_map/between/pallas_call | solution.py:362
  154.1 3.6 %collective-permute-start.10 = (f32[48,768]{1,0:T(8,128)}, f32[48,768]{1,0:T(8,128)S(1)}, u32[]{:S(2)}, u32[]{:S(2)}) collective-permute-start(f32[48,768]{1,0:T(8,128)} %get-tuple-element.25.a), channel_id=1, source_target_pairs={{0,1},{1,0},{2,3},{3,2},{4,5},{5,4},{6,7},{7,6},{8,9},{9,8},{10,11... | collective-permute-start | bytes 442376 | tf_op jit(solution)/shard_map/ppermute | solution.py:451
  157.7 6.7 %collective-permute-done.10.b = f32[48,768]{1,0:T(8,128)S(1)} collective-permute-done((f32[48,768]{1,0:T(8,128)}, f32[48,768]{1,0:T(8,128)S(1)}, u32[]{:S(2)}, u32[]{:S(2)}) %collective-permute-start.10) | collective-permute-done | bytes 147488 | tf_op jit(solution)/shard_map/ppermute | solution.py:451
  164.4 0.0 copy-start.8
  164.4 0.0 collective-permute-done.9
  164.4 0.0 copy-done.5
  164.4 0.1 add.7.mine
  164.5 0.0 copy-start.6
  164.5 2.1 collective-permute-start.11
  166.6 1.9 collective-permute-done.11.theirs
  168.6 0.0 copy-done.8
  168.6 0.0 copy-done.6
  168.6 0.0 copy-start.7
  168.6 0.9 copy-done.7
  169.5 37.2 %level_two.1 = f32[96,768]{1,0:T(8,128)} custom-call(f32[128,1408]{1,0:T(8,128)} %copy-done.6, f32[128,1408]{1,0:T(8,128)} %copy-done.7, f32[768,768]{1,0:T(8,128)} %get-tuple-element.23.m, f32[48,768]{1,0:T(8,128)} %get-tuple-element.24.base, f32[48,768]{1,0:T(8,128)} %get-tuple-element.25.a, f32[48,768]{1,0:T(8,128)} %copy-done.8, s32[1,768]{1,0:T(1,128)} %copy-done.3), custom_call_target="tpu_custom_call" | custom-call | flops 40000000000 | bytes 12000000 | tf_op jit(solution)/shard_map/level_two/pallas_call | solution.py:417
  206.7 3.1 %collective-permute-start.12 = (f32[96,768]{1,0:T(8,128)}, f32[96,768]{1,0:T(8,128)S(1)}, u32[]{:S(2)}, u32[]{:S(2)}) collective-permute-start(f32[96,768]{1,0:T(8,128)} %level_two.1), channel_id=1, source_target_pairs={{0,1},{1,0},{2,3},{3,2},{4,5},{5,4},{6,7},{7,6},{8,9},{9,8},{10,11... | collective-permute-start | bytes 884744 | tf_op jit(solution)/shard_map/ppermute | solution.py:456
  209.8 8.0 %collective-permute-done.12 = f32[96,768]{1,0:T(8,128)S(1)} collective-permute-done((f32[96,768]{1,0:T(8,128)}, f32[96,768]{1,0:T(8,128)S(1)}, u32[]{:S(2)}, u32[]{:S(2)}) %collective-permute-start.12) | collective-permute-done | bytes 294944 | tf_op jit(solution)/shard_map/ppermute | solution.py:456
  217.8 1.8 fusion
  (8 shorter events, 0.1 us)
Async XLA Ops:
  7.2 125.1 %all-gather.2.cloned.1.call-start = ((), (), s32[]{:S(2)}) async-start(), calls=%async_computation | async-start | bytes 9732096 | tf_op jit(solution)/shard_map/all_gather | solution.py:439
  7.9 82.5 %copy-start.3 = (s32[1,768]{1,0:T(1,128)}, s32[1,768]{1,0:T(1,128)S(1)}, u32[]{:S(2)}) copy-start(s32[1,768]{1,0:T(1,128)S(1)} %reshape.9.ro) | copy-start | bytes 9220
  7.9 0.9 copy-start
  8.8 0.9 copy-start.1
  9.7 0.9 copy-start.2
  13.4 19.9 %collective-permute-start = (f32[48,768]{1,0:T(8,128)S(1)}, f32[48,768]{1,0:T(8,128)S(1)}, u32[]{:S(2)}, u32[]{:S(2)}) collective-permute-start(f32[48,768]{1,0:T(8,128)S(1)} %get-tuple-element.15), channel_id=1, source_target_pairs={{0,4},{4,0},{1,5},{5,1},{2,6},{6,2},{3,7},{7,3},{8,12},{12,8},{9,1... | collective-permute-start | bytes 442376 | tf_op jit(solution)/shard_map/ppermute | solution.py:440
  33.3 21.4 %collective-permute-start.1 = (f32[48,768]{1,0:T(8,128)S(1)}, f32[48,768]{1,0:T(8,128)S(1)}, u32[]{:S(2)}, u32[]{:S(2)}) collective-permute-start(f32[48,768]{1,0:T(8,128)S(1)} %get-tuple-element.28), channel_id=1, source_target_pairs={{64,0},{128,64},{192,128},{256,192},{320,256},{384,320},{448,384},... | collective-permute-start | bytes 442376 | tf_op jit(solution)/shard_map/ppermute | solution.py:432
  54.7 13.0 %collective-permute-start.2 = (f32[48,768]{1,0:T(8,128)S(1)}, f32[48,768]{1,0:T(8,128)S(1)}, u32[]{:S(2)}, u32[]{:S(2)}) collective-permute-start(f32[48,768]{1,0:T(8,128)S(1)} %collective-permute-done.1), channel_id=1, source_target_pairs={{64,0},{128,64},{192,128},{256,192},{320,256},{384,320},{448,384},... | collective-permute-start | bytes 442376 | tf_op jit(solution)/shard_map/ppermute | solution.py:432
  62.2 11.4 %collective-permute-start.5 = (f32[48,768]{1,0:T(8,128)S(1)}, f32[48,768]{1,0:T(8,128)S(1)}, u32[]{:S(2)}, u32[]{:S(2)}) collective-permute-start(f32[48,768]{1,0:T(8,128)S(1)} %get-tuple-element.28), channel_id=1, source_target_pairs={{452,0},{0,64},{64,128},{128,192},{192,256},{256,320},{320,384},{3... | collective-permute-start | bytes 442376 | tf_op jit(solution)/shard_map/ppermute | solution.py:432
  67.7 11.6 %collective-permute-start.3 = (f32[48,768]{1,0:T(8,128)S(1)}, f32[48,768]{1,0:T(8,128)S(1)}, u32[]{:S(2)}, u32[]{:S(2)}) collective-permute-start(f32[48,768]{1,0:T(8,128)S(1)} %collective-permute-done.2), channel_id=1, source_target_pairs={{64,0},{128,64},{192,128},{256,192},{320,256},{384,320},{448,384},... | collective-permute-start | bytes 442376 | tf_op jit(solution)/shard_map/ppermute | solution.py:432
  73.7 11.5 %collective-permute-start.6 = (f32[48,768]{1,0:T(8,128)S(1)}, f32[48,768]{1,0:T(8,128)S(1)}, u32[]{:S(2)}, u32[]{:S(2)}) collective-permute-start(f32[48,768]{1,0:T(8,128)S(1)} %collective-permute-done.5), channel_id=1, source_target_pairs={{452,0},{0,64},{64,128},{128,192},{192,256},{256,320},{320,384},{3... | collective-permute-start | bytes 442376 | tf_op jit(solution)/shard_map/ppermute | solution.py:432
  79.3 11.1 %collective-permute-start.4 = (f32[48,768]{1,0:T(8,128)S(1)}, f32[48,768]{1,0:T(8,128)S(1)}, u32[]{:S(2)}, u32[]{:S(2)}) collective-permute-start(f32[48,768]{1,0:T(8,128)S(1)} %collective-permute-done.3), channel_id=1, source_target_pairs={{64,0},{128,64},{192,128},{256,192},{320,256},{384,320},{448,384},... | collective-permute-start | bytes 442376 | tf_op jit(solution)/shard_map/ppermute | solution.py:432
  85.1 11.3 %collective-permute-start.7 = (f32[48,768]{1,0:T(8,128)S(1)}, f32[48,768]{1,0:T(8,128)S(1)}, u32[]{:S(2)}, u32[]{:S(2)}) collective-permute-start(f32[48,768]{1,0:T(8,128)S(1)} %collective-permute-done.6), channel_id=1, source_target_pairs={{452,0},{0,64},{64,128},{128,192},{192,256},{256,320},{320,384},{3... | collective-permute-start | bytes 442376 | tf_op jit(solution)/shard_map/ppermute | solution.py:432
  96.5 5.0 %collective-permute-start.8 = (f32[384,768]{1,0:T(8,128)S(1)}, f32[384,768]{1,0:T(8,128)S(1)}, u32[]{:S(2)}, u32[]{:S(2)}) collective-permute-start(f32[384,768]{1,0:T(8,128)S(1)} %constant_dynamic-update-slice_fusion.mine), channel_id=1, source_target_pairs={{0,32},{32,0},{1,33},{33,1},{2,34},{34,2},{3,35},{35,3},{4,36},{36... | collective-permute-start | bytes 3538952 | tf_op jit(solution)/shard_map/ppermute | solution.py:447
  130.8 1.5 copy-start.4
  140.5 23.9 %collective-permute-start.9 = (f32[128,1408]{1,0:T(8,128)}, f32[128,1408]{1,0:T(8,128)S(1)}, u32[]{:S(2)}, u32[]{:S(2)}) collective-permute-start(f32[128,1408]{1,0:T(8,128)} %get-tuple-element.17), channel_id=1, source_target_pairs={{0,1},{1,0},{2,3},{3,2},{4,5},{5,4},{6,7},{7,6},{8,9},{9,8},{10,11... | collective-permute-start | bytes 2162696 | tf_op jit(solution)/shard_map/ppermute | solution.py:449
  144.8 19.6 %copy-start.5 = (f32[128,1408]{1,0:T(8,128)S(1)}, f32[128,1408]{1,0:T(8,128)}, u32[]{:S(2)}) copy-start(f32[128,1408]{1,0:T(8,128)} %get-tuple-element.17) | copy-start | bytes 2162692
  154.1 10.3 %collective-permute-start.10 = (f32[48,768]{1,0:T(8,128)}, f32[48,768]{1,0:T(8,128)S(1)}, u32[]{:S(2)}, u32[]{:S(2)}) collective-permute-start(f32[48,768]{1,0:T(8,128)} %get-tuple-element.25.a), channel_id=1, source_target_pairs={{0,1},{1,0},{2,3},{3,2},{4,5},{5,4},{6,7},{7,6},{8,9},{9,8},{10,11... | collective-permute-start | bytes 442376 | tf_op jit(solution)/shard_map/ppermute | solution.py:451
  164.4 4.2 %copy-start.8 = (f32[48,768]{1,0:T(8,128)}, f32[48,768]{1,0:T(8,128)S(1)}, u32[]{:S(2)}) copy-start(f32[48,768]{1,0:T(8,128)S(1)} %collective-permute-done.10.b) | copy-start | bytes 442372
  164.5 4.1 %copy-start.6 = (f32[128,1408]{1,0:T(8,128)}, f32[128,1408]{1,0:T(8,128)S(1)}, u32[]{:S(2)}) copy-start(f32[128,1408]{1,0:T(8,128)S(1)} %add.7.mine) | copy-start | bytes 2162692
  164.5 4.1 %collective-permute-start.11 = (f32[128,1408]{1,0:T(8,128)S(1)}, f32[128,1408]{1,0:T(8,128)S(1)}, u32[]{:S(2)}, u32[]{:S(2)}) collective-permute-start(f32[128,1408]{1,0:T(8,128)S(1)} %add.7.mine), channel_id=1, source_target_pairs={{0,32},{32,0},{1,33},{33,1},{2,34},{34,2},{3,35},{35,3},{4,36},{36... | collective-permute-start | bytes 2162696 | tf_op jit(solution)/shard_map/ppermute | solution.py:454
  168.6 0.9 copy-start.7
  206.7 11.2 %collective-permute-start.12 = (f32[96,768]{1,0:T(8,128)}, f32[96,768]{1,0:T(8,128)S(1)}, u32[]{:S(2)}, u32[]{:S(2)}) collective-permute-start(f32[96,768]{1,0:T(8,128)} %level_two.1), channel_id=1, source_target_pairs={{0,1},{1,0},{2,3},{3,2},{4,5},{5,4},{6,7},{7,6},{8,9},{9,8},{10,11... | collective-permute-start | bytes 884744 | tf_op jit(solution)/shard_map/ppermute | solution.py:456
Sparse Core Ops, SparseCore 0:
  13.5 95.7 all-gather.1

commit v3 on v2

v3 whole, which is shorter than its diff:
```python
import functools

import jax
import jax.numpy as jnp
from jax import lax
from jax.experimental import pallas as pl
from jax.experimental.pallas import tpu as pltpu
from jax.sharding import Mesh
from jax.sharding import PartitionSpec as P

F = 768
ROWS = 48
CHUNKED = (16, 2, 24, 768)
B = 128
F32 = jnp.float32
BF16 = jnp.bfloat16
PAIR = ("zh", "zl", "core")
SWAP = [(0, 1), (1, 0)]
VMEM = pl.BlockSpec(memory_space=pltpu.VMEM)
HBM = pl.BlockSpec(memory_space=pltpu.HBM)


def params(mib):
    return pltpu.CompilerParams(vmem_limit_bytes=mib * 1024 * 1024)


def dg(a, b, dims):
    return lax.dot_general(a, b, (dims, ((), ())), preferred_element_type=F32)


NN = ((1,), (0,))
NT = ((1,), (1,))
TN = ((0,), (0,))
TT = ((0,), (1,))


def split3(x):
    h = x.astype(BF16)
    y = x - h.astype(F32)
    m = y.astype(BF16)
    return h, m, (y - m.astype(F32)).astype(BF16)


def mul6(a, b, dims):
    low = (dg(a[2], b[0], dims) + dg(a[0], b[2], dims)) + dg(a[1], b[1], dims)
    return (low + (dg(a[1], b[0], dims) + dg(a[0], b[1], dims))) + dg(a[0], b[0], dims)


def chunks(body):
    def one(j, carry):
        body(pl.ds(pl.multiple_of(j * 256, 256), 256))
        return carry

    lax.fori_loop(0, F // 256, one, 0)


def mul_into(out_ref, x_ref, y_ref, parts):
    for ref, piece in zip(parts, split3(x_ref[...])):
        ref[...] = piece

    def tile(js):
        out_ref[:, js] = mul6([ref[...] for ref in parts], split3(y_ref[:, js]), NN)

    chunks(tile)


def pick(x, onehot, dims):
    h, m, l = split3(x)
    return (dg(l, onehot, dims) + dg(m, onehot, dims)) + dg(h, onehot, dims)


def pick_nt(e, x):
    h, m, l = split3(x)
    return (dg(e, l, NT) + dg(e, m, NT)) + dg(e, h, NT)


def onehot_of(ro):
    c = lax.broadcasted_iota(jnp.int32, (F, F), 0)
    return jnp.where(c == ro, 1.0, 0.0).astype(BF16)


def sub(v, s):
    return jnp.broadcast_to(v[s : s + 1, :], v.shape)


def lane(v, j):
    return jnp.broadcast_to(v[:, j : j + 1], v.shape)


def inv8(b, row):
    b = list(b)
    for p in range(4):
        i, k = 2 * p, 2 * p + 1
        a_, b_, d_ = sub(b[i], i), sub(b[k], i), sub(b[k], k)
        rd = 1.0 / (a_ * d_ - b_ * b_)
        pa, pb, pd = d_ * rd, -b_ * rd, a_ * rd
        ci = jnp.where(row == i, -1.0, jnp.where(row == k, 0.0, b[i]))
        ck = jnp.where(row == k, -1.0, jnp.where(row == i, 0.0, b[k]))
        ui = ci * pa + ck * pb
        uk = ci * pb + ck * pd
        keep = (row != i) & (row != k)
        new = []
        for j in range(8):
            if j == i:
                new.append(-ui)
            elif j == k:
                new.append(-uk)
            else:
                base = jnp.where(keep, b[j], 0.0)
                new.append(base - (ui * sub(b[j], i) + uk * sub(b[j], k)))
        b = new
    return b


def tree(u):
    return ((u[0] + u[1]) + (u[2] + u[3])) + ((u[4] + u[5]) + (u[6] + u[7]))


def inv128(D):
    row = lax.broadcasted_iota(jnp.int32, (8, B), 0)
    col = lax.broadcasted_iota(jnp.int32, (8, B), 1)
    D = list(D)
    for r in range(16):
        rows = D[r]
        ib = inv8([lane(rows, 8 * r + j) for j in range(8)], row)
        inp = (col >= 8 * r) & (col < 8 * r + 8)
        rows = jnp.where(inp, jnp.where(col - 8 * r == row, 1.0, 0.0), rows)
        T = tree([ib[j] * sub(rows, j) for j in range(8)])
        Tj = [sub(T, j) for j in range(8)]
        for q in list(range(r + 1, 16)) + list(range(r)):
            u = tree([lane(D[q], 8 * r + j) * Tj[j] for j in range(8)])
            D[q] = jnp.where(inp, 0.0, D[q]) - u
        D[r] = T
    return D


def cat(*a, axis):
    return jnp.concatenate(a, axis=axis)


def stack6(a):
    a0, a1, a2 = split3(a)
    return cat(a0, a1, axis=1), cat(a0, a2, axis=1)


def mul128(a, b):
    b0, b1, b2 = split3(b)
    low = dg(a[1], cat(b2, b0, axis=0), NN) + dg(a[0], cat(b1, b1, axis=0), NN)
    return low + dg(a[0], cat(b0, b0, axis=0), NN)


def invert(s_ref, d_ref, di_ref, r_ref, c_ref):
    ri = lax.broadcasted_iota(jnp.int32, (B, B), 0)
    ci = lax.broadcasted_iota(jnp.int32, (B, B), 1)
    eye = jnp.where(ri == ci, 1.0, 0.0)
    last = F // B - 1
    di_ref[...] = jnp.zeros((B, B), F32)
    r_ref[...] = jnp.zeros((B, F), F32)
    c_ref[...] = jnp.zeros((F, B), F32)
    d_ref[...] = s_ref[:B, :B]

    def trail(kp):
        T = mul128(stack6(di_ref[...]), r_ref[...])
        c = stack6(c_ref[...])
        for j in range(F // 256):
            js = slice(256 * j, 256 * j + 256)
            s_ref[:F, js] = s_ref[:F, js] - mul128(c, T[:, js])
        s_ref[pl.ds(kp, B), :] = T

    def finish(kp):
        r_ref[...] = mul128(stack6(di_ref[...]), r_ref[...])

        def tile(js):
            s_ref[:F, js] = s_ref[:F, js] - mul128(stack6(c_ref[...]), r_ref[:, js])

        chunks(tile)
        s_ref[pl.ds(kp, B), :] = r_ref[...]

    def step(k, carry):
        ks = pl.multiple_of(k * B, B)
        kp = pl.multiple_of(jnp.where(k == 0, F, ks - B), B)
        kn = pl.multiple_of(jnp.where(k == last, F - B, ks + B), B)
        Di = jnp.concatenate(inv128([d_ref[8 * q : 8 * q + 8, :] for q in range(16)]), axis=0)
        trail(kp)
        rn = s_ref[pl.ds(ks, B), pl.ds(kn, B)]
        cn = s_ref[pl.ds(kn, B), pl.ds(ks, B)]
        dn = s_ref[pl.ds(kn, B), pl.ds(kn, B)]
        c_ref[...] = s_ref[:F, pl.ds(ks, B)]
        c_ref[pl.ds(ks, B), :] = jnp.zeros((B, B), F32)
        r_ref[...] = s_ref[pl.ds(ks, B), :]
        r_ref[:, pl.ds(ks, B)] = eye
        s_ref[:F, pl.ds(ks, B)] = jnp.zeros((F, B), F32)
        di_ref[...] = Di
        d_ref[...] = dn - mul128(stack6(cn), mul128(stack6(Di), rn))
        return carry

    lax.fori_loop(0, last + 1, step, 0)
    finish(F - B)


INVERT_SCRATCH = [
    pltpu.VMEM((F + B, F), F32),
    pltpu.VMEM((B, B), F32),
    pltpu.VMEM((B, B), F32),
    pltpu.VMEM((B, F), F32),
    pltpu.VMEM((F, B), F32),
]


def enter_body(ro, left, cross, right, cross_out, part):
    p = onehot_of(ro[...])
    upper = lax.axis_index("zh") == 1
    l, c, r = left[...], cross[...], right[...]
    part[:ROWS, :] = pick(jnp.where(upper, l, r), p, NN)
    part[ROWS:, :] = pick(jnp.where(upper, r, l), p, NN)
    cross_out[...] = pick(c, p, NN)


def enter(ro, left, cross, right):
    return pl.pallas_call(
        enter_body,
        out_shape=(jax.ShapeDtypeStruct((ROWS, F), F32), jax.ShapeDtypeStruct((2 * ROWS, F), F32)),
        in_specs=[VMEM] * 4,
        out_specs=(VMEM, VMEM),
        compiler_params=params(32),
        name="enter",
    )(ro, left, cross, right)


def level_one_body(mine, theirs, si_out, s_ref, *work):
    core = lax.axis_index("core")
    zl = lax.axis_index("zl")
    for k in range(8):
        at = lax.rem(zl + k, 8) * (2 * ROWS)
        s_ref[pl.ds(pl.multiple_of(at + core * ROWS, ROWS), ROWS), :] = mine[ROWS * k : ROWS * k + ROWS, :]
        s_ref[pl.ds(pl.multiple_of(at + (1 - core) * ROWS, ROWS), ROWS), :] = theirs[ROWS * k : ROWS * k + ROWS, :]
    invert(s_ref, *work)
    si_out[...] = s_ref[:F, :]


def level_one(mine, theirs):
    return pl.pallas_call(
        level_one_body,
        out_shape=jax.ShapeDtypeStruct((F, F), F32),
        in_specs=[VMEM, VMEM],
        out_specs=VMEM,
        scratch_shapes=INVERT_SCRATCH,
        compiler_params=params(56),
        cost_estimate=pl.CostEstimate(flops=40 * 10**9, transcendentals=0, bytes_accessed=5 * 10**6),
        name="level_one",
    )(mine, theirs)


def rows_copy(g, chunk, box, dst, sem):
    return pltpu.make_async_copy(g.at[chunk, box], dst, sem)


def products_body(si, g, w_out, t_out, x4, y4, o4, t_ref, x0, x1, x2, sems):
    low = lax.axis_index("xl") == 0
    first = lax.axis_index("core") == 0
    x_ref, y_ref, o_ref = (r.reshape(F, F) for r in (x4, y4, o4))

    @pl.when(low)
    def _():
        for j in range(2):
            rows_copy(g, j, 1, y4.at[:, j], sems.at[j]).start()
        x_ref[...] = si[...]

    @pl.when(jnp.logical_not(low))
    def _():
        for j in range(2):
            rows_copy(g, j, 0, x4.at[:, j], sems.at[j]).start()
        y_ref[...] = si[...]

    for z in range(2):
        rows_copy(g, 2, z, o4.at[:, z], sems.at[2 + z]).start()
    for j in range(2):
        rows_copy(g, j, 0, x4.at[:, j], sems.at[j]).wait()
    mul_into(t_ref, x_ref, y_ref, (x0, x1, x2))
    out = pltpu.make_async_copy(t_ref, t_out, sems.at[0])
    out.start()
    for z in range(2):
        rows_copy(g, 2, z, o4.at[:, z], sems.at[2 + z]).wait()

    def panels(term):
        def fill(places):
            w_out[...] = jnp.zeros((B, 11 * B), F32)
            for i, at in places:
                w_out[:, at : at + F - B * i] = o_ref[B * i : B * i + B, B * i :]

            def part(ks):
                for i, at in places:
                    here = slice(at, at + F - B * i)
                    w_out[:, here] = w_out[:, here] - term(i, ks)

            chunks(part)

        @pl.when(first)
        def _():
            fill(((0, 0), (1, 768)))

        @pl.when(jnp.logical_not(first))
        def _():
            fill(((2, 0), (3, 512), (4, 896), (5, 1152)))

    @pl.when(low)
    def _():
        panels(lambda i, ks: mul6(split3(y_ref[ks, B * i : B * i + B]), split3(t_ref[ks, B * i :]), TN))

    @pl.when(jnp.logical_not(low))
    def _():
        panels(
            lambda i, ks: mul6(
                split3(t_ref[B * i : B * i + B, ks]), [ref[B * i :, ks] for ref in (x0, x1, x2)], NT
            )
        )

    out.wait()


def products(si, g):
    return pl.pallas_call(
        products_body,
        out_shape=(jax.ShapeDtypeStruct((B, 11 * B), F32), jax.ShapeDtypeStruct((F, F), F32)),
        in_specs=[VMEM, HBM],
        out_specs=(VMEM, HBM),
        scratch_shapes=[pltpu.VMEM(CHUNKED, F32)] * 3
        + [pltpu.VMEM((F, F), F32)]
        + [pltpu.VMEM((F, F), BF16)] * 3
        + [pltpu.SemaphoreType.DMA((4,))],
        compiler_params=params(56),
        cost_estimate=pl.CostEstimate(flops=6 * 10**9, transcendentals=0, bytes_accessed=12 * 10**6),
        name="products",
    )(si, g)


def between_body(g, t, si, keep, m_out, base_out, a_out, x4, y4, m_ref, x0, x1, x2, sems):
    low = lax.axis_index("xl") == 0
    i = (lax.axis_index("zl") * 2 + lax.axis_index("core")) * ROWS
    i = pl.multiple_of(i, ROWS)
    x_ref, y_ref = x4.reshape(F, F), y4.reshape(F, F)

    @pl.when(low)
    def _():
        for j in range(2):
            rows_copy(g, j, 0, x4.at[:, j], sems.at[j]).start()
        pltpu.make_async_copy(t, y4, sems.at[2]).start()

    @pl.when(jnp.logical_not(low))
    def _():
        pltpu.make_async_copy(t, x4, sems.at[2]).start()
        for j in range(2):
            rows_copy(g, j, 1, y4.at[:, j], sems.at[j]).start()

    for j in range(2):
        rows_copy(g, j, 0, x4.at[:, j], sems.at[j]).wait()
    pltpu.make_async_copy(t, x4, sems.at[2]).wait()
    parts = (x0, x1, x2)
    mul_into(m_ref, x_ref, y_ref, parts)
    out = pltpu.make_async_copy(m_ref, m_out, sems.at[0])
    out.start()
    zero = jnp.zeros((ROWS, F), F32)

    def times_inverse(rows):
        a_out[...] = zero

        def part(ks):
            a_out[...] = a_out[...] + mul6(rows(ks), split3(si[ks, :]), NN)

        chunks(part)

    base_out[...] = keep[...]

    @pl.when(low)
    def _():
        times_inverse(lambda ks: [ref[pl.ds(i, ROWS), ks] for ref in parts])

        def part(ks):
            base_out[...] = base_out[...] - mul6(split3(a_out[:, ks]), [ref[:, ks] for ref in parts], NT)

        chunks(part)
        a_out[...] = m_ref[pl.ds(i, ROWS), :]

    @pl.when(jnp.logical_not(low))
    def _():
        r_ = lax.broadcasted_iota(jnp.int32, (ROWS, F), 0) + i
        c_ = lax.broadcasted_iota(jnp.int32, (ROWS, F), 1)
        e = jnp.where(r_ == c_, 1.0, 0.0).astype(BF16)
        times_inverse(lambda ks: [dg(e, p, NT).astype(BF16) for p in split3(y_ref[ks, :])])

        def part(ks):
            base_out[...] = base_out[...] - mul6(split3(a_out[:, ks]), split3(y_ref[ks, :]), NN)

        chunks(part)
        a_out[...] = pick_nt(e, m_ref[...])

    out.wait()


def between(g, t, si, keep):
    rows = jax.ShapeDtypeStruct((ROWS, F), F32)
    return pl.pallas_call(
        between_body,
        out_shape=(jax.ShapeDtypeStruct((F, F), F32), rows, rows),
        in_specs=[HBM, HBM, VMEM, VMEM],
        out_specs=(HBM, VMEM, VMEM),
        scratch_shapes=[pltpu.VMEM(CHUNKED, F32)] * 2
        + [pltpu.VMEM((F, F), F32)]
        + [pltpu.VMEM((F, F), BF16)] * 3
        + [pltpu.SemaphoreType.DMA((3,))],
        compiler_params=params(56),
        cost_estimate=pl.CostEstimate(flops=6 * 10**9, transcendentals=0, bytes_accessed=12 * 10**6),
        name="between",
    )(g, t.reshape(CHUNKED), si, keep)


def level_two_body(mine, theirs, m, base, a, b, ro, out, m_ref, y_ref, z_ref, sems, s_ref, *work):
    gm = pltpu.make_async_copy(m, m_ref, sems.at[0])
    gm.start()
    first = lax.axis_index("core") == 0
    upper = jnp.where(first, mine[...], theirs[...])
    lower = jnp.where(first, theirs[...], mine[...])
    rows = [
        upper[:, :768],
        upper[:, 768:],
        lower[:, :512],
        lower[:, 512:896],
        lower[:, 896:1152],
        lower[:, 1152:1280],
    ]
    for i in range(6):
        s_ref[B * i : B * i + B, B * i :] = rows[i]
        for j in range(i + 1, 6):
            s_ref[B * j : B * j + B, B * i : B * i + B] = rows[i][:, B * (j - i) : B * (j - i) + B].T
    invert(s_ref, *work)
    gm.wait()
    low = lax.axis_index("xl") == 0
    x = jnp.concatenate([jnp.where(low, a[...], b[...]), a[...]], axis=0)
    xs = split3(x)
    y_ref[...] = mul6(xs, split3(s_ref[:F, :]), NN)

    @pl.when(low)
    def _():
        z_ref[...] = mul6(split3(y_ref[...]), split3(m_ref[...]), NT)

    @pl.when(jnp.logical_not(low))
    def _():
        z_ref[...] = mul6(split3(y_ref[...]), split3(m_ref[...]), NN)

    top = jnp.where(low, base[...], 0.0) - z_ref[:ROWS, :]
    bottom = base[...] - z_ref[ROWS:, :]
    p = onehot_of(ro[...])
    out[...] = pick(jnp.concatenate([top, bottom], axis=0), p, NT)


def level_two(mine, theirs, m, base, a, b, ro):
    return pl.pallas_call(
        level_two_body,
        out_shape=jax.ShapeDtypeStruct((2 * ROWS, F), F32),
        in_specs=[VMEM, VMEM, HBM, VMEM, VMEM, VMEM, VMEM],
        out_specs=VMEM,
        scratch_shapes=[pltpu.VMEM((F, F), F32)]
        + [pltpu.VMEM((2 * ROWS, F), F32)] * 2
        + [pltpu.SemaphoreType.DMA((1,))]
        + INVERT_SCRATCH,
        compiler_params=params(56),
        cost_estimate=pl.CostEstimate(flops=40 * 10**9, transcendentals=0, bytes_accessed=12 * 10**6),
        name="level_two",
    )(mine, theirs, m, base, a, b, ro)


def shift(x, by):
    at = lambda z: z % 8 * 2 + z // 8
    return lax.ppermute(x, ("zl", "zh"), [(at((z + by) % 16), at(z)) for z in range(16)])


def shards(row_owner, face_left, face_cross, face_right):
    ro = row_owner.reshape(1, F)
    xl = lax.axis_index("xl")
    zh = lax.axis_index("zh")
    cross, part = enter(ro, face_left[0, 0], face_cross[0, 0], face_right[0, 0])
    partner = lax.ppermute(part, "zh", SWAP)
    mine = part[:ROWS] + partner[:ROWS]
    middle = jnp.where(zh == xl, partner[ROWS:], part[ROWS:])
    keep = jnp.where(zh == xl, part[ROWS:], partner[ROWS:])
    middle = jnp.where(zh == 0, middle[:24], middle[24:])
    g = lax.all_gather(jnp.concatenate([cross, middle]).reshape(3, 24, F), PAIR, axis=1, tiled=True)
    g = g.reshape(3, 2, 16, 24, F)
    ups, downs = [mine], [mine]
    for _ in range(4):
        ups.append(shift(ups[-1], 1))
        if len(downs) < 4:
            downs.append(shift(downs[-1], -1))
    pieces = jnp.concatenate(ups + downs[:0:-1], axis=0)
    si = level_one(pieces, lax.ppermute(pieces, "core", SWAP))
    w, t = products(si, g)
    w2 = lax.ppermute(w, "xl", SWAP)
    m, base, a = between(g, t, si, keep)
    b = lax.ppermute(a, "xl", SWAP)
    w2, m, base, a, b = lax.optimization_barrier((w2, m, base, a, b))
    w = w + w2
    w2 = lax.ppermute(w, "core", SWAP)
    mine = level_two(w, w2, m, base, a, b, ro)
    theirs = lax.ppermute(mine, "xl", SWAP)
    low = xl == 0
    left = jnp.where(low, mine[:ROWS], theirs[:ROWS])
    cross = jnp.where(low, theirs[:ROWS], mine[:ROWS])
    right = jnp.where(low, theirs[ROWS:], mine[ROWS:])
    return (left[None, None], cross[None, None], right[None, None])


def solution(mesh):
    fine = Mesh(mesh.devices.reshape(8, 2, 4, 2, 2, 2), ("zl", "core", "y", "zh", "xh", "xl"))
    face = P(("y", "zh"), ("xh", "xl"), ("zl", "core"), None)
    return jax.shard_map(
        shards, mesh=fine, in_specs=(P(), face, face, face), out_specs=(face, face, face), check_vma=False
    )
```

time: 227 us -> 248 us (1.093)
  Pallas kernels: 86.8 us -> 104 us
  starting transfers between devices: 67.4 us -> 72.3 us
    ppermute x1, waiting for transfers between devices: 4.13 us -> 11.5 us  [shards(): partner = lax.ppermute(part, 'zh', SWAP)]
    ppermute x7, waiting for transfers between devices: 26.4 us -> 19.4 us  [shift(): lax.ppermute(x, ('zl', 'zh'), [(at((z + by) % 16), at(z)) for z in range(...]
    pallas_call x1, Pallas kernels: 9.26 us -> 15.6 us  [between(): pl.pallas_call(between_body, out_shape=(jax.ShapeDtypeStruct((F, F), F32)...]
    pallas_call x1, Pallas kernels: 8.26 us -> 13.7 us  [products(): pl.pallas_call(products_body, out_shape=(jax.ShapeDtypeStruct((B, 11 * B)...]
    pallas_call x1, Pallas kernels: 29.4 us -> 34.3 us  [level_one(): pl.pallas_call(level_one_body, out_shape=jax.ShapeDtypeStruct((F, F), F32...]
    ppermute x7, starting transfers between devices: 36.6 us -> 40 us  [shift(): lax.ppermute(x, ('zl', 'zh'), [(at((z + by) % 16), at(z)) for z in range(...]
    ppermute x1, waiting for transfers between devices: 6.7 us -> 4.08 us  [shards(): b = lax.ppermute(a, 'xl', SWAP)]
    unnamed x24 -> x26, local copies, waits for them, and re-layouts: 5.16 us -> 4.81 us
  transfers between devices with their start and end apart: 14 -> 14, of which waited for: 12 -> 11; matrix products, arithmetic and copies ran while one was open for 0% -> 0% of each run, Pallas kernels for 17% -> 20%
where the time goes in v3:
time: 248 us
  Pallas kernels  104 us (42%)
  starting transfers between devices  72.3 us (29%)
  waiting for transfers between devices  48.4 us (20%)
  between operations  14.3 us (6%)
  local copies, waits for them, and re-layouts  5.51 us (2%)
  other arithmetic  3.25 us (1%)
    ppermute x7, starting transfers between devices, shift(): lax.ppermute(x, ('zl', 'zh'), [(at((z + by) % 16), at(z)) for z in range(...  40 us
    pallas_call x1, Pallas kernels, level_two(): pl.pallas_call(level_two_body, out_shape=jax.ShapeDtypeStruct((2 * ROWS,...  38.3 us
    pallas_call x1, Pallas kernels, level_one(): pl.pallas_call(level_one_body, out_shape=jax.ShapeDtypeStruct((F, F), F32...  34.3 us
    ppermute x7, waiting for transfers between devices, shift(): lax.ppermute(x, ('zl', 'zh'), [(at((z + by) % 16), at(z)) for z in range(...  19.4 us
    ppermute x1, starting transfers between devices, shards(): partner = lax.ppermute(part, 'zh', SWAP)  15.7 us
    pallas_call x1, Pallas kernels, between(): pl.pallas_call(between_body, out_shape=(jax.ShapeDtypeStruct((F, F), F32)...  15.6 us
    pallas_call x1, Pallas kernels, products(): pl.pallas_call(products_body, out_shape=(jax.ShapeDtypeStruct((B, 11 * B)...  13.7 us
    ppermute x1, waiting for transfers between devices, shards(): partner = lax.ppermute(part, 'zh', SWAP)  11.5 us
  transfers between devices with their start and end apart: 14, of which 11 were waited for; matrix products, arithmetic and copies ran while one was open for 0% of the time, Pallas kernels for 20%

profile of v3, /device:TPU:24, one launch (start us, length us, event | category | flops | bytes accessed | tf_op | source)
XLA Modules:
  0.0 247.5 jit_solution(395717752505374523)
XLA Ops:
  7.2 0.0 all-gather.2.cloned.1.call-start
  7.2 0.7 reshape.18.ro
  7.9 0.0 copy-start.3
  7.9 0.0 copy-start
  7.9 0.9 copy-done
  8.8 0.0 copy-start.1
  8.8 0.9 copy-done.1
  9.7 0.0 copy-start.2
  9.7 0.9 copy-done.2
  10.6 2.0 enter.1
  12.6 15.7 %collective-permute-start = (f32[96,768]{1,0:T(8,128)S(1)}, f32[96,768]{1,0:T(8,128)S(1)}, u32[]{:S(2)}, u32[]{:S(2)}) collective-permute-start(f32[96,768]{1,0:T(8,128)S(1)} %get-tuple-element.15), channel_id=1, source_target_pairs={{0,4},{4,0},{1,5},{5,1},{2,6},{6,2},{3,7},{7,3},{8,12},{12,8},{9,1... | collective-permute-start | bytes 884744 | tf_op jit(solution)/shard_map/ppermute | solution.py:482
  28.4 11.5 %collective-permute-done = f32[96,768]{1,0:T(8,128)S(1)} collective-permute-done((f32[96,768]{1,0:T(8,128)S(1)}, f32[96,768]{1,0:T(8,128)S(1)}, u32[]{:S(2)}, u32[]{:S(2)}) %collective-permute-start) | collective-permute-done | bytes 294944 | tf_op jit(solution)/shard_map/ppermute | solution.py:482
  39.9 0.7 slice_select_fusion.1
  40.6 0.7 pad_maximum_fusion
  41.3 0.0 all-gather.2.cloned.1.call-update
  41.3 0.0 copy-done.3
  41.4 15.2 %collective-permute-start.1 = (f32[48,768]{1,0:T(8,128)S(1)}, f32[48,768]{1,0:T(8,128)S(1)}, u32[]{:S(2)}, u32[]{:S(2)}) collective-permute-start(f32[48,768]{1,0:T(8,128)S(1)} %get-tuple-element.35), channel_id=1, source_target_pairs={{64,0},{128,64},{192,128},{256,192},{320,256},{384,320},{448,384},... | collective-permute-start | bytes 442376 | tf_op jit(solution)/shard_map/ppermute | solution.py:474
  56.6 5.0 %collective-permute-done.1 = f32[48,768]{1,0:T(8,128)S(1)} collective-permute-done((f32[48,768]{1,0:T(8,128)S(1)}, f32[48,768]{1,0:T(8,128)S(1)}, u32[]{:S(2)}, u32[]{:S(2)}) %collective-permute-start.1) | collective-permute-done | bytes 147488 | tf_op jit(solution)/shard_map/ppermute | solution.py:474
  61.5 7.8 %collective-permute-start.2 = (f32[48,768]{1,0:T(8,128)S(1)}, f32[48,768]{1,0:T(8,128)S(1)}, u32[]{:S(2)}, u32[]{:S(2)}) collective-permute-start(f32[48,768]{1,0:T(8,128)S(1)} %collective-permute-done.1), channel_id=1, source_target_pairs={{64,0},{128,64},{192,128},{256,192},{320,256},{384,320},{448,384},... | collective-permute-start | bytes 442376 | tf_op jit(solution)/shard_map/ppermute | solution.py:474
  69.4 1.9 collective-permute-start.5
  71.3 0.7 collective-permute-done.2
  72.0 5.6 %collective-permute-start.3 = (f32[48,768]{1,0:T(8,128)S(1)}, f32[48,768]{1,0:T(8,128)S(1)}, u32[]{:S(2)}, u32[]{:S(2)}) collective-permute-start(f32[48,768]{1,0:T(8,128)S(1)} %collective-permute-done.2), channel_id=1, source_target_pairs={{64,0},{128,64},{192,128},{256,192},{320,256},{384,320},{448,384},... | collective-permute-start | bytes 442376 | tf_op jit(solution)/shard_map/ppermute | solution.py:474
  77.6 2.0 collective-permute-done.5
  79.6 1.9 collective-permute-start.6
  81.6 1.3 collective-permute-done.3
  82.9 5.6 %collective-permute-start.4 = (f32[48,768]{1,0:T(8,128)S(1)}, f32[48,768]{1,0:T(8,128)S(1)}, u32[]{:S(2)}, u32[]{:S(2)}) collective-permute-start(f32[48,768]{1,0:T(8,128)S(1)} %collective-permute-done.3), channel_id=1, source_target_pairs={{64,0},{128,64},{192,128},{256,192},{320,256},{384,320},{448,384},... | collective-permute-start | bytes 442376 | tf_op jit(solution)/shard_map/ppermute | solution.py:474
  88.5 2.1 collective-permute-done.6
  90.6 1.9 collective-permute-start.7
  92.6 0.0 collective-permute-done.4
  92.6 8.3 %collective-permute-done.7 = f32[48,768]{1,0:T(8,128)S(1)} collective-permute-done((f32[48,768]{1,0:T(8,128)S(1)}, f32[48,768]{1,0:T(8,128)S(1)}, u32[]{:S(2)}, u32[]{:S(2)}) %collective-permute-start.7) | collective-permute-done | bytes 147488 | tf_op jit(solution)/shard_map/ppermute | solution.py:474
  100.9 0.0 copy-start.6
  100.9 1.9 collective-permute-start.8
  102.9 3.1 %collective-permute-done.8.theirs = f32[384,768]{1,0:T(8,128)S(1)} collective-permute-done((f32[384,768]{1,0:T(8,128)S(1)}, f32[384,768]{1,0:T(8,128)S(1)}, u32[]{:S(2)}, u32[]{:S(2)}) %collective-permute-start.8) | collective-permute-done | bytes 1179680 | tf_op jit(solution)/shard_map/ppermute | solution.py:495
  105.9 0.0 copy-done.6
  105.9 0.0 copy-start.7
  105.9 1.1 copy-done.7
  107.0 34.3 %level_one.1.si = f32[768,768]{1,0:T(8,128)} custom-call(f32[384,768]{1,0:T(8,128)} %copy-done.6, f32[384,768]{1,0:T(8,128)} %copy-done.7), custom_call_target="tpu_custom_call" | custom-call | flops 40000000000 | bytes 5000000 | tf_op jit(solution)/shard_map/level_one/pallas_call | solution.py:242
  141.3 0.0 all-gather.2.cloned.1.call-done
  141.3 13.7 %products.1 = (f32[128,1408]{1,0:T(8,128)}, f32[768,768]{1,0:T(8,128)}) custom-call(f32[768,768]{1,0:T(8,128)} %level_one.1.si, f32[3,2,16,24,768]{4,3,2,1,0:T(8,128)} %bitcast.16), custom_call_target="tpu_custom_call" | custom-call | flops 6000000000 | bytes 12000000 | tf_op jit(solution)/shard_map/products/pallas_call | solution.py:322
  154.9 5.0 %collective-permute-start.9 = (f32[128,1408]{1,0:T(8,128)}, f32[128,1408]{1,0:T(8,128)S(1)}, u32[]{:S(2)}, u32[]{:S(2)}) collective-permute-start(f32[128,1408]{1,0:T(8,128)} %get-tuple-element.17), channel_id=1, source_target_pairs={{0,1},{1,0},{2,3},{3,2},{4,5},{5,4},{6,7},{7,6},{8,9},{9,8},{10,11... | collective-permute-start | bytes 2162696 | tf_op jit(solution)/shard_map/ppermute | solution.py:497
  160.0 0.0 copy-start.4
  160.0 15.6 %between.1 = (f32[768,768]{1,0:T(8,128)}, f32[48,768]{1,0:T(8,128)}, f32[48,768]{1,0:T(8,128)}) custom-call(f32[3,2,16,24,768]{4,3,2,1,0:T(8,128)} %bitcast.17, f32[16,2,24,768]{3,2,1,0:T(8,128)} %bitcast.18, f32[768,768]{1,0:T(8,128)} %level_one.1.si, f32[48,768]{1,0:T(8,128)} %get-tuple-element.32.keep), custom_call_target="tpu_custom_call" | custom-call | flops 6000000000 | bytes 12000000 | tf_op jit(solution)/shard_map/between/pallas_call | solution.py:402
  175.6 4.7 %collective-permute-start.10 = (f32[48,768]{1,0:T(8,128)}, f32[48,768]{1,0:T(8,128)S(1)}, u32[]{:S(2)}, u32[]{:S(2)}) collective-permute-start(f32[48,768]{1,0:T(8,128)} %get-tuple-element.25.a), channel_id=1, source_target_pairs={{0,1},{1,0},{2,3},{3,2},{4,5},{5,4},{6,7},{7,6},{8,9},{9,8},{10,11... | collective-permute-start | bytes 442376 | tf_op jit(solution)/shard_map/ppermute | solution.py:499
  180.3 4.1 %collective-permute-done.10.b = f32[48,768]{1,0:T(8,128)S(1)} collective-permute-done((f32[48,768]{1,0:T(8,128)}, f32[48,768]{1,0:T(8,128)S(1)}, u32[]{:S(2)}, u32[]{:S(2)}) %collective-permute-start.10) | collective-permute-done | bytes 147488 | tf_op jit(solution)/shard_map/ppermute | solution.py:499
  184.4 0.0 copy-start.9
  184.4 0.0 collective-permute-done.9
  184.4 0.0 copy-done.4
  184.4 0.1 add.7.mine
  184.5 0.0 copy-start.5
  184.5 2.1 collective-permute-start.11
  186.6 1.9 collective-permute-done.11.theirs
  188.6 0.0 copy-done.9
  188.6 0.0 copy-done.5
  188.6 0.0 copy-start.8
  188.6 0.9 copy-done.8
  189.5 38.3 %level_two.1 = f32[96,768]{1,0:T(8,128)} custom-call(f32[128,1408]{1,0:T(8,128)} %copy-done.5, f32[128,1408]{1,0:T(8,128)} %copy-done.8, f32[768,768]{1,0:T(8,128)} %get-tuple-element.23.m, f32[48,768]{1,0:T(8,128)} %get-tuple-element.24.base, f32[48,768]{1,0:T(8,128)} %get-tuple-element.25.a, f32[48,768]{1,0:T(8,128)} %copy-done.9, s32[1,768]{1,0:T(1,128)} %copy-done.3), custom_call_target="tpu_custom_call" | custom-call | flops 40000000000 | bytes 12000000 | tf_op jit(solution)/shard_map/level_two/pallas_call | solution.py:457
  227.8 2.7 %collective-permute-start.12 = (f32[96,768]{1,0:T(8,128)}, f32[96,768]{1,0:T(8,128)S(1)}, u32[]{:S(2)}, u32[]{:S(2)}) collective-permute-start(f32[96,768]{1,0:T(8,128)} %level_two.1), channel_id=1, source_target_pairs={{0,1},{1,0},{2,3},{3,2},{4,5},{5,4},{6,7},{7,6},{8,9},{9,8},{10,11... | collective-permute-start | bytes 884744 | tf_op jit(solution)/shard_map/ppermute | solution.py:504
  230.5 8.4 %collective-permute-done.12 = f32[96,768]{1,0:T(8,128)S(1)} collective-permute-done((f32[96,768]{1,0:T(8,128)}, f32[96,768]{1,0:T(8,128)S(1)}, u32[]{:S(2)}, u32[]{:S(2)}) %collective-permute-start.12) | collective-permute-done | bytes 294944 | tf_op jit(solution)/shard_map/ppermute | solution.py:504
  238.9 1.8 fusion
  (8 shorter events, 0.1 us)
Async XLA Ops:
  7.2 134.1 %all-gather.2.cloned.1.call-start = ((), (), s32[]{:S(2)}) async-start(), calls=%async_computation | async-start | bytes 7299072 | tf_op jit(solution)/shard_map/all_gather | solution.py:487
  7.9 33.4 %copy-start.3 = (s32[1,768]{1,0:T(1,128)}, s32[1,768]{1,0:T(1,128)S(1)}, u32[]{:S(2)}) copy-start(s32[1,768]{1,0:T(1,128)S(1)} %reshape.18.ro) | copy-start | bytes 9220
  7.9 0.9 copy-start
  8.8 0.9 copy-start.1
  9.7 0.9 copy-start.2
  12.6 27.3 %collective-permute-start = (f32[96,768]{1,0:T(8,128)S(1)}, f32[96,768]{1,0:T(8,128)S(1)}, u32[]{:S(2)}, u32[]{:S(2)}) collective-permute-start(f32[96,768]{1,0:T(8,128)S(1)} %get-tuple-element.15), channel_id=1, source_target_pairs={{0,4},{4,0},{1,5},{5,1},{2,6},{6,2},{3,7},{7,3},{8,12},{12,8},{9,1... | collective-permute-start | bytes 884744 | tf_op jit(solution)/shard_map/ppermute | solution.py:482
  41.4 20.2 %collective-permute-start.1 = (f32[48,768]{1,0:T(8,128)S(1)}, f32[48,768]{1,0:T(8,128)S(1)}, u32[]{:S(2)}, u32[]{:S(2)}) collective-permute-start(f32[48,768]{1,0:T(8,128)S(1)} %get-tuple-element.35), channel_id=1, source_target_pairs={{64,0},{128,64},{192,128},{256,192},{320,256},{384,320},{448,384},... | collective-permute-start | bytes 442376 | tf_op jit(solution)/shard_map/ppermute | solution.py:474
  61.5 10.5 %collective-permute-start.2 = (f32[48,768]{1,0:T(8,128)S(1)}, f32[48,768]{1,0:T(8,128)S(1)}, u32[]{:S(2)}, u32[]{:S(2)}) collective-permute-start(f32[48,768]{1,0:T(8,128)S(1)} %collective-permute-done.1), channel_id=1, source_target_pairs={{64,0},{128,64},{192,128},{256,192},{320,256},{384,320},{448,384},... | collective-permute-start | bytes 442376 | tf_op jit(solution)/shard_map/ppermute | solution.py:474
  69.4 10.2 %collective-permute-start.5 = (f32[48,768]{1,0:T(8,128)S(1)}, f32[48,768]{1,0:T(8,128)S(1)}, u32[]{:S(2)}, u32[]{:S(2)}) collective-permute-start(f32[48,768]{1,0:T(8,128)S(1)} %get-tuple-element.35), channel_id=1, source_target_pairs={{452,0},{0,64},{64,128},{128,192},{192,256},{256,320},{320,384},{3... | collective-permute-start | bytes 442376 | tf_op jit(solution)/shard_map/ppermute | solution.py:474
  72.0 10.8 %collective-permute-start.3 = (f32[48,768]{1,0:T(8,128)S(1)}, f32[48,768]{1,0:T(8,128)S(1)}, u32[]{:S(2)}, u32[]{:S(2)}) collective-permute-start(f32[48,768]{1,0:T(8,128)S(1)} %collective-permute-done.2), channel_id=1, source_target_pairs={{64,0},{128,64},{192,128},{256,192},{320,256},{384,320},{448,384},... | collective-permute-start | bytes 442376 | tf_op jit(solution)/shard_map/ppermute | solution.py:474
  79.6 11.0 %collective-permute-start.6 = (f32[48,768]{1,0:T(8,128)S(1)}, f32[48,768]{1,0:T(8,128)S(1)}, u32[]{:S(2)}, u32[]{:S(2)}) collective-permute-start(f32[48,768]{1,0:T(8,128)S(1)} %collective-permute-done.5), channel_id=1, source_target_pairs={{452,0},{0,64},{64,128},{128,192},{192,256},{256,320},{320,384},{3... | collective-permute-start | bytes 442376 | tf_op jit(solution)/shard_map/ppermute | solution.py:474
  82.9 9.7 %collective-permute-start.4 = (f32[48,768]{1,0:T(8,128)S(1)}, f32[48,768]{1,0:T(8,128)S(1)}, u32[]{:S(2)}, u32[]{:S(2)}) collective-permute-start(f32[48,768]{1,0:T(8,128)S(1)} %collective-permute-done.3), channel_id=1, source_target_pairs={{64,0},{128,64},{192,128},{256,192},{320,256},{384,320},{448,384},... | collective-permute-start | bytes 442376 | tf_op jit(solution)/shard_map/ppermute | solution.py:474
  90.6 10.2 %collective-permute-start.7 = (f32[48,768]{1,0:T(8,128)S(1)}, f32[48,768]{1,0:T(8,128)S(1)}, u32[]{:S(2)}, u32[]{:S(2)}) collective-permute-start(f32[48,768]{1,0:T(8,128)S(1)} %collective-permute-done.6), channel_id=1, source_target_pairs={{452,0},{0,64},{64,128},{128,192},{192,256},{256,320},{320,384},{3... | collective-permute-start | bytes 442376 | tf_op jit(solution)/shard_map/ppermute | solution.py:474
  100.9 5.0 %copy-start.6 = (f32[384,768]{1,0:T(8,128)}, f32[384,768]{1,0:T(8,128)S(1)}, u32[]{:S(2)}) copy-start(f32[384,768]{1,0:T(8,128)S(1)} %constant_dynamic-update-slice_fusion.mine) | copy-start | bytes 3538948
  100.9 5.0 %collective-permute-start.8 = (f32[384,768]{1,0:T(8,128)S(1)}, f32[384,768]{1,0:T(8,128)S(1)}, u32[]{:S(2)}, u32[]{:S(2)}) collective-permute-start(f32[384,768]{1,0:T(8,128)S(1)} %constant_dynamic-update-slice_fusion.mine), channel_id=1, source_target_pairs={{0,32},{32,0},{1,33},{33,1},{2,34},{34,2},{3,35},{35,3},{4,36},{36... | collective-permute-start | bytes 3538952 | tf_op jit(solution)/shard_map/ppermute | solution.py:495
  105.9 1.1 copy-start.7
  154.9 29.4 %collective-permute-start.9 = (f32[128,1408]{1,0:T(8,128)}, f32[128,1408]{1,0:T(8,128)S(1)}, u32[]{:S(2)}, u32[]{:S(2)}) collective-permute-start(f32[128,1408]{1,0:T(8,128)} %get-tuple-element.17), channel_id=1, source_target_pairs={{0,1},{1,0},{2,3},{3,2},{4,5},{5,4},{6,7},{7,6},{8,9},{9,8},{10,11... | collective-permute-start | bytes 2162696 | tf_op jit(solution)/shard_map/ppermute | solution.py:497
  160.0 24.4 %copy-start.4 = (f32[128,1408]{1,0:T(8,128)S(1)}, f32[128,1408]{1,0:T(8,128)}, u32[]{:S(2)}) copy-start(f32[128,1408]{1,0:T(8,128)} %get-tuple-element.17) | copy-start | bytes 2162692
  175.6 8.8 %collective-permute-start.10 = (f32[48,768]{1,0:T(8,128)}, f32[48,768]{1,0:T(8,128)S(1)}, u32[]{:S(2)}, u32[]{:S(2)}) collective-permute-start(f32[48,768]{1,0:T(8,128)} %get-tuple-element.25.a), channel_id=1, source_target_pairs={{0,1},{1,0},{2,3},{3,2},{4,5},{5,4},{6,7},{7,6},{8,9},{9,8},{10,11... | collective-permute-start | bytes 442376 | tf_op jit(solution)/shard_map/ppermute | solution.py:499
  184.4 4.2 %copy-start.9 = (f32[48,768]{1,0:T(8,128)}, f32[48,768]{1,0:T(8,128)S(1)}, u32[]{:S(2)}) copy-start(f32[48,768]{1,0:T(8,128)S(1)} %collective-permute-done.10.b) | copy-start | bytes 442372
  184.5 4.1 %copy-start.5 = (f32[128,1408]{1,0:T(8,128)}, f32[128,1408]{1,0:T(8,128)S(1)}, u32[]{:S(2)}) copy-start(f32[128,1408]{1,0:T(8,128)S(1)} %add.7.mine) | copy-start | bytes 2162692
  184.5 4.1 %collective-permute-start.11 = (f32[128,1408]{1,0:T(8,128)S(1)}, f32[128,1408]{1,0:T(8,128)S(1)}, u32[]{:S(2)}, u32[]{:S(2)}) collective-permute-start(f32[128,1408]{1,0:T(8,128)S(1)} %add.7.mine), channel_id=1, source_target_pairs={{0,32},{32,0},{1,33},{33,1},{2,34},{34,2},{3,35},{35,3},{4,36},{36... | collective-permute-start | bytes 2162696 | tf_op jit(solution)/shard_map/ppermute | solution.py:502
  188.6 0.9 copy-start.8
  227.8 11.1 %collective-permute-start.12 = (f32[96,768]{1,0:T(8,128)}, f32[96,768]{1,0:T(8,128)S(1)}, u32[]{:S(2)}, u32[]{:S(2)}) collective-permute-start(f32[96,768]{1,0:T(8,128)} %level_two.1), channel_id=1, source_target_pairs={{0,1},{1,0},{2,3},{3,2},{4,5},{5,4},{6,7},{7,6},{8,9},{9,8},{10,11... | collective-permute-start | bytes 884744 | tf_op jit(solution)/shard_map/ppermute | solution.py:504
Sparse Core Ops, SparseCore 0:
  41.5 94.8 all-gather.1
